TPU v7x, 128 devices: a whole 4x4x4 slice. The times are simulated.
128 devices in a mesh: pair: 2 (over x_hi), seq: 32 (over z, y, core), head: 2 (over x_lo).
Axes of the slice: x: 4 (x_hi: 2, x_lo: 2; x = x_hi * 2 + x_lo), y: 4, z: 4, core: 2. Of those that a mesh axis runs over, the one named last changes fastest.
Arguments:
- queries: bfloat16 [2, 2048, 2, 3584], P('pair', 'seq', None, 'head'), may hold values from -6 to 6
- answer_keys: bfloat16 [2, 2048, 2, 512], P('pair', 'seq', None, 'head'), may hold values from -6 to 6
- answer_values: bfloat16 [2, 2048, 2, 512], P('pair', 'seq', None, 'head'), may hold values from -6 to 6
- prefix_keys: bfloat16 [3072, 512], P(('pair', 'seq'), 'head'), may hold values from -8 to 8
- prefix_values: bfloat16 [3072, 512], P(('pair', 'seq'), 'head'), may hold values from -6 to 6
- grad_out: bfloat16 [2, 2048, 2, 3584], P('pair', 'seq', None, 'head'), may hold values from -6 to 6
- answer_length: int32 [2, 2], P('pair'), may hold values from 512 to 2048
- prefix_limit: int32 [2, 2], P('pair'), may hold values from 1536 to 3072
Outputs:
- attention_out: bfloat16 [2, 2048, 2, 3584], P('pair', 'seq', None, 'head')
- grad_queries: bfloat16 [2, 2048, 2, 3584], P('pair', 'seq', None, 'head')
- grad_answer_keys: bfloat16 [2, 2048, 2, 512], P('pair', 'seq', None, 'head')
- grad_answer_values: bfloat16 [2, 2048, 2, 512], P('pair', 'seq', None, 'head')
- grad_prefix_keys: float32 [3072, 512], P(('pair', 'seq'), 'head')
- grad_prefix_values: float32 [3072, 512], P(('pair', 'seq'), 'head')
All inputs are finite; a program needn't handle non-finite values.
Results may differ from a plain program's by a relative error of at most 0.015.
Values may be sent and summed in bfloat16 or wider, within the bound.
A program may use at most 64 MiB of HBM per device.

v0:
```python
import jax
import jax.numpy as jnp
from jax import lax
from jax.sharding import PartitionSpec as P

HEAD_DIM = 128


negative_fill = -1e30
prefix_forms = ("rbkgd,jkd->bkgrj", "bkgrj,jkd->rbkgd", "bkgrj,rbkgd->jkd")
answer_forms = ("rbkgd,jbkd->bkgrj", "bkgrj,jbkd->rbkgd", "bkgrj,rbkgd->jbkd")


def side_by_side(arrays, axis, dim, along):
    both = jnp.concatenate(arrays, axis=along)
    filled, at, finished = (lax.all_gather(both, axis, axis=dim, tiled=True), 0, [])
    for a in arrays:
        finished.append(lax.slice_in_dim(filled, at, at + a.shape[along], axis=along))
        at += a.shape[along]
    return tuple(finished)


def in_blocks(value, dim, peers):
    before, after = (value.shape[:dim], value.shape[dim + 1 :])
    return jnp.moveaxis(value.reshape(*before, peers, -1, *after), dim, 0)


def sum_at_owner(value, axis, dim):
    peers = lax.axis_size(axis)
    blocks = lax.all_to_all(in_blocks(value, dim, peers), axis, 0, 0, tiled=True)
    return jnp.sum(blocks.astype(jnp.float32), axis=0)


def block_width(row_total):
    block_rows = min(row_total, 512)
    while row_total % block_rows != 0:
        block_rows = block_rows - 1
    return block_rows


def sweep_keys(update, carried, key_rows, value_rows):
    block_rows = block_width(key_rows.shape[0])
    blocks_total = key_rows.shape[0] // block_rows
    key_blocks = key_rows.reshape((blocks_total, block_rows) + key_rows.shape[1:])
    value_blocks = value_rows.reshape((blocks_total, block_rows) + value_rows.shape[1:])
    starts = jnp.arange(blocks_total, dtype=jnp.int32) * block_rows

    def advance(running, inputs):
        return update(running, inputs[0], inputs[1], inputs[2])

    return lax.scan(advance, carried, (key_blocks, value_blocks, starts))


def prefix_allowed(limits):

    def prefix_allowed_keys(first, key_span):
        places = first + lax.iota(jnp.int32, key_span)
        return (places[None, :] < limits[:, None])[:, None, None, None, :]

    return prefix_allowed_keys


def answer_allowed(row_places):

    def answer_allowed_keys(first, key_span):
        places = first + lax.iota(jnp.int32, key_span)
        return (places[None, :] <= row_places[:, None])[None, None, None]

    return answer_allowed_keys


def make_scorer(forms, query_view, allow_rule):
    scaling = query_view.shape[-1] ** (-0.5)

    def scorer(key_block, first):
        raw_scores = (
            jnp.einsum(forms[0], query_view, key_block, preferred_element_type=jnp.float32)
            * scaling
        )
        return (raw_scores, allow_rule(first, key_block.shape[0]))

    return scorer


def stats_step(scorer):

    def update(running, key_block, value_block, first):
        top_score, exp_total = running
        raw_scores, allowed = scorer(key_block, first)
        masked = jnp.where(allowed, raw_scores, negative_fill)
        new_top = jnp.maximum(top_score, jnp.max(masked, axis=-1))
        block_sum = jnp.sum(jnp.where(allowed, jnp.exp(masked - new_top[..., None]), 0.0), axis=-1)
        return ((new_top, exp_total * jnp.exp(top_score - new_top) + block_sum), None)

    return update


def output_step(scorer, forms, log_total):

    def update(running, key_block, value_block, first):
        raw_scores, allowed = scorer(key_block, first)
        probs_low = jnp.where(allowed, jnp.exp(raw_scores - log_total[..., None]), 0.0).astype(
            jnp.bfloat16
        )
        return (
            running
            + jnp.einsum(forms[1], probs_low, value_block, preferred_element_type=jnp.float32),
            None,
        )

    return update


def backward_step(scorer, forms, query_view, douts, log_total, delta):
    scaling = query_view.shape[-1] ** (-0.5)

    def update(carried, key_block, value_block, first):
        raw_scores, allowed = scorer(key_block, first)
        probs = jnp.where(allowed, jnp.exp(raw_scores - log_total[..., None]), 0.0)
        grad_probs = jnp.einsum(forms[0], douts, value_block, preferred_element_type=jnp.float32)
        grad_low = (probs * (grad_probs - delta[..., None])).astype(jnp.bfloat16)
        terms = None
        key_term = (
            jnp.einsum(forms[2], grad_low, query_view, preferred_element_type=jnp.float32) * scaling
        )
        value_term = jnp.einsum(
            forms[2], probs.astype(jnp.bfloat16), douts, preferred_element_type=jnp.float32
        )
        flat_key = key_term.reshape(key_term.shape[:-2] + (-1,))
        flat_value = value_term.reshape(value_term.shape[:-2] + (-1,))
        terms = jnp.concatenate([flat_key, flat_value], axis=-1)
        carried = carried + jnp.einsum(
            forms[1], grad_low, key_block, preferred_element_type=jnp.float32
        )
        return (carried, terms)

    return update


def on_device(
    queries,
    answer_keys,
    answer_values,
    prefix_keys,
    prefix_values,
    grad_out,
    answer_length,
    prefix_limit,
):
    rows_here = queries.shape[1]
    batch_here = queries.shape[2]
    head_size = HEAD_DIM
    kv_local = answer_keys.shape[3] // head_size
    group_size = queries.shape[3] // head_size // kv_local
    feature_width = kv_local * head_size
    view_shape = (rows_here, batch_here, kv_local, group_size, head_size)
    query_view = queries[0].reshape(view_shape)
    row_places = lax.axis_index("seq") * rows_here + lax.iota(jnp.int32, rows_here)
    live_rows = (row_places[:, None] < answer_length[0][None, :])[:, :, None, None, None]
    douts = jnp.where(
        live_rows, grad_out[0].reshape(view_shape), jnp.zeros(view_shape, jnp.bfloat16)
    )
    prefix_whole = side_by_side((prefix_keys, prefix_values), ("pair", "seq"), 0, 1)
    prefix_total = prefix_whole[0].shape[0]
    prefix_key_rows = prefix_whole[0].reshape(prefix_total, kv_local, head_size)
    prefix_value_rows = prefix_whole[1].reshape(prefix_total, kv_local, head_size)
    answer_whole = side_by_side((answer_keys[0], answer_values[0]), "seq", 0, 1)
    answer_total = answer_whole[0].shape[0]
    answer_key_rows = answer_whole[0].reshape(answer_total, batch_here, kv_local, head_size)
    answer_value_rows = answer_whole[1].reshape(answer_total, batch_here, kv_local, head_size)
    prefix_scorer = make_scorer(prefix_forms, query_view, prefix_allowed(prefix_limit[0]))
    answer_scorer = make_scorer(answer_forms, query_view, answer_allowed(row_places))
    stat_shape = (batch_here, kv_local, group_size, rows_here)
    running = (jnp.full(stat_shape, negative_fill, jnp.float32), jnp.zeros(stat_shape, jnp.float32))
    running, _ = sweep_keys(stats_step(prefix_scorer), running, prefix_key_rows, prefix_value_rows)
    running, _ = sweep_keys(stats_step(answer_scorer), running, answer_key_rows, answer_value_rows)
    log_total = running[0] + jnp.log(running[1])
    attended = jnp.zeros(view_shape, jnp.float32)
    attended, _ = sweep_keys(
        output_step(prefix_scorer, prefix_forms, log_total),
        attended,
        prefix_key_rows,
        prefix_value_rows,
    )
    attended, _ = sweep_keys(
        output_step(answer_scorer, answer_forms, log_total),
        attended,
        answer_key_rows,
        answer_value_rows,
    )
    attended = jnp.where(live_rows, attended, 0.0)
    attention_out = attended.astype(jnp.bfloat16).reshape(queries.shape)
    delta = jnp.transpose(jnp.sum(douts.astype(jnp.float32) * attended, axis=-1), (1, 2, 3, 0))
    grad_acc = jnp.zeros(view_shape, jnp.float32)
    both_sides = backward_step(prefix_scorer, prefix_forms, query_view, douts, log_total, delta)
    grad_acc, terms = sweep_keys(both_sides, grad_acc, prefix_key_rows, prefix_value_rows)
    partial_terms = terms.reshape(prefix_total, -1)
    halves = sum_at_owner(partial_terms.astype(jnp.bfloat16), "pair", 0)
    prefix_sums = sum_at_owner(halves.astype(jnp.bfloat16), "seq", 0)
    answer_side = backward_step(answer_scorer, answer_forms, query_view, douts, log_total, delta)
    grad_acc, answer_terms = sweep_keys(answer_side, grad_acc, answer_key_rows, answer_value_rows)
    answer_sums = lax.psum_scatter(
        answer_terms.reshape(answer_total, batch_here, -1).astype(jnp.bfloat16),
        "seq",
        scatter_dimension=0,
        tiled=True,
    ).astype(jnp.float32)
    grad_queries = (grad_acc * head_size ** (-0.5)).astype(jnp.bfloat16).reshape(queries.shape)
    grad_answer_keys = (
        answer_sums[:, :, :feature_width].astype(jnp.bfloat16).reshape(answer_keys.shape)
    )
    grad_answer_values = (
        answer_sums[:, :, feature_width:].astype(jnp.bfloat16).reshape(answer_values.shape)
    )
    grad_prefix_keys = prefix_sums[:, :feature_width]
    grad_prefix_values = prefix_sums[:, feature_width:]
    return (
        attention_out,
        grad_queries,
        grad_answer_keys,
        grad_answer_values,
        grad_prefix_keys,
        grad_prefix_values,
    )


def solution(mesh):
    return jax.shard_map(
        on_device,
        mesh=mesh,
        in_specs=(
            P("pair", "seq", None, "head"),
            P("pair", "seq", None, "head"),
            P("pair", "seq", None, "head"),
            P(("pair", "seq"), "head"),
            P(("pair", "seq"), "head"),
            P("pair", "seq", None, "head"),
            P("pair", None),
            P("pair", None),
        ),
        out_specs=(
            P("pair", "seq", None, "head"),
            P("pair", "seq", None, "head"),
            P("pair", "seq", None, "head"),
            P("pair", "seq", None, "head"),
            P(("pair", "seq"), "head"),
            P(("pair", "seq"), "head"),
        ),
        check_vma=False,
    )
```

profile of v0, /device:TPU:1, one launch (start us, length us, event | category | flops | bytes accessed | tf_op | source)
XLA Modules:
  0.0 472.1 jit_solution(8770837318021649274)
XLA Ops:
  13.4 71.7 %all-gather.3.cloned.1.call-done = bf16[3072,512]{1,0:T(8,128)(2,1)} async-done(((bf16[48,512]{1,0:T(8,128)(2,1)}), bf16[3072,512]{1,0:T(8,128)(2,1)}) %all-gather.3.cloned.1.call-update) | async-done | bytes 3145744 | tf_op jit(solution)/shard_map/all_gather | solution.py:16
  85.2 3.3 fusion.105
  88.4 1.9 reshape_reshape.9
  92.0 19.6 %while.77 = (s32[]{:T(128)}, f32[2,2,7,64]{3,2,0,1:T(8,128)S(1)}, f32[2,2,7,64]{3,2,0,1:T(8,128)S(1)}, s32[6]{0:T(128)S(1)}, s32[1,2]{1,0:T(1,128)S(1)}, /*index...) while((s32[]{:T(128)}, f32[2,2,7,64]{3,2,0,1:T(8,128)S(1)}, ...), condition=%wide.region_3.4_spmd.clone, body=%wide.region_0.3_spmd.clone.sunk | while | flops 242231552 | bytes 8162444 | solution.py:51
  111.6 3.8 reshape_reshape.8
  115.4 2.8 copy.126
  118.2 13.7 %all-gather.5.cloned.1.call-done = bf16[2048,4,256]{2,1,0:T(4,128)(2,1)} async-done(((bf16[64,4,256]{2,1,0:T(4,128)(2,1)}), bf16[2048,4,256]{2,1,0:T(4,128)(2,1)}) %all-gather.5.cloned.1.call-update) | async-done | bytes 4194320 | tf_op jit(solution)/shard_map/all_gather | solution.py:16
  131.9 8.0 %fusion.104 = (bf16[2048,2,256]{2,1,0:T(2,128)(2,1)}, bf16[2048,2,256]{2,1,0:T(2,128)(2,1)}) fusion(bf16[2048,4,256]{2,1,0:T(4,128)(2,1)} %all-gather.5.cloned.1.call-done), kind=kLoop, calls=%fused_computation.139 | loop fusion | bytes 8388608 | tf_op jit(solution)/shard_map/slice | solution.py:18
  139.9 6.0 %reshape.290 = bf16[4,512,2,2,128]{4,3,2,1,0:T(2,128)(2,1)S(1)} reshape(bf16[2048,2,256]{2,1,0:T(2,128)(2,1)} %get-tuple-element.760) | data formatting | bytes 4194304 | tf_op jit(solution)/shard_map/reshape;reshape | solution.py:45
  147.7 6.8 %reshape.289 = bf16[4,512,2,2,128]{4,3,2,1,0:T(2,128)(2,1)} reshape(bf16[2048,2,256]{2,1,0:T(2,128)(2,1)} %get-tuple-element.761) | data formatting | bytes 4194304 | tf_op jit(solution)/shard_map/reshape;reshape | solution.py:44
  154.5 2.0 copy.122
  156.6 13.5 %while.74 = (s32[]{:T(128)}, f32[2,2,7,64]{3,2,1,0:T(8,128)S(1)}, f32[2,2,7,64]{3,2,1,0:T(8,128)S(1)}, s32[4]{0:T(128)S(1)}, bf16[4,512,2,2,128]{4,1,3,2,0:T(8,1...) while((s32[]{:T(128)}, f32[2,2,7,64]{3,2,1,0:T(8,128)S(1)}, ...), condition=%wide.region_7.8_spmd.clone, body=%wide.region_4.7_spmd.clone.sunk | while | flops 242257984 | bytes 8519285 | solution.py:51
  170.1 29.5 %while.78 = (s32[]{:T(128)}, f32[64,2,2,7,128]{4,0,3,1,2:T(8,128)}, bf16[6,512,2,128]{3,1,2,0:T(8,128)(2,1)}, s32[6]{0:T(128)S(1)}, s32[1,2]{1,0:T(1,128)S(1)}, ...) while((s32[]{:T(128)}, f32[64,2,2,7,128]{4,0,3,1,2:T(8,128)}, ...), condition=%wide.region_9.10_spmd.clone, body=%wide.region_8.9_spmd.clone.sunk | while | flops 473892352 | bytes 2833038 | solution.py:51
  171.4 3.4 fusion.190
  176.1 3.6 fusion.190
  181.0 3.6 fusion.190
  186.0 3.6 fusion.190
  191.0 3.6 fusion.190
  195.9 3.6 fusion.190
  199.6 2.2 copy.130
  201.8 19.7 %while.75 = (s32[]{:T(128)}, f32[64,2,2,7,128]{4,0,3,2,1:T(8,128)}, bf16[4,512,2,2,128]{4,1,3,2,0:T(8,128)(2,1)}, s32[4]{0:T(128)S(1)}, bf16[4,512,2,2,128]{4,1,...) while((s32[]{:T(128)}, f32[64,2,2,7,128]{4,0,3,2,1:T(8,128)}, ...), condition=%wide.region_11.12_spmd.clone, body=%wide.region_10.11_spmd.clone.sunk | while | flops 473694784 | bytes 3430009 | solution.py:51
  203.1 3.6 fusion.167
  208.1 3.6 fusion.167
  213.0 3.6 fusion.167
  217.9 3.6 fusion.167
  221.5 3.5 multiply_reduce_fusion
  225.0 3.0 copy_select_fusion.1
  230.0 1.9 copy.140
  232.0 55.8 %while.79 = (s32[]{:T(128)}, f32[64,2,2,7,128]{4,0,3,1,2:T(8,128)S(1)}, bf16[6,512,512]{2,1,0:T(8,128)(2,1)}, bf16[6,512,2,128]{3,1,2,0:T(8,128)(2,1)}, s32[6]{0...) while((s32[]{:T(128)}, ...), condition=%wide.region_14.15_spmd.clone, body=%wide.region_13.14_spmd.clone.sunk | while | flops 1185351168 | bytes 26505428 | solution.py:51
  235.1 2.2 fusion.200
  242.6 1.8 fusion.199
  244.5 2.2 fusion.200
  251.9 1.8 fusion.199
  253.8 2.2 fusion.200
  263.1 2.2 fusion.200
  272.4 2.2 fusion.200
  279.8 1.8 fusion.199
  281.7 2.2 fusion.200
  287.8 5.5 %all-to-all-start = ((bf16[2,1536,512]{2,1,0:T(8,128)(2,1)}), bf16[2,1536,512]{2,1,0:T(8,128)(2,1)}, u32[]{:S(2)}, u32[]{:S(2)}) async-start(bf16[2,1536,512]{2,1,0:T(8,128)(2,1)} %bitcast.360), calls=%async_computation | async-start | bytes 6291456 | tf_op jit(solution)/shard_map/all_to_all | solution.py:30
  294.7 31.6 %while.76 = (s32[]{:T(128)}, f32[64,2,2,7,128]{4,0,3,2,1:T(8,128)S(1)}, bf16[4,512,2,512]{1,3,2,0:T(8,128)(2,1)}, bf16[4,512,2,2,128]{4,1,3,2,0:T(8,128)(2,1)S(1...) while((s32[]{:T(128)}, ...), condition=%wide.region_16.17_spmd.clone, body=%wide.region_15.16_spmd.clone.sunk | while | flops 1186464256 | bytes 26863292 | solution.py:51
  297.8 2.4 fusion.179
  305.6 2.4 fusion.179
  313.5 2.4 fusion.179
  321.4 2.4 fusion.179
  326.3 11.1 %copy.150 = bf16[4,512,2,512]{3,2,1,0:T(2,128)(2,1)} copy(bf16[4,512,2,512]{1,3,2,0:T(8,128)(2,1)} %get-tuple-element.290) | data formatting | bytes 8388608 | tf_op jit(solution)/shard_map/convert_element_type | solution.py:203
  337.5 4.1 reduce_sum.49
  341.6 5.3 %all-to-all-start.1 = ((bf16[32,48,512]{2,1,0:T(8,128)(2,1)}), bf16[32,48,512]{2,1,0:T(8,128)(2,1)S(1)}, u32[]{:S(2)}, u32[]{:S(2)}) async-start(bf16[32,48,512]{2,1,0:T(8,128)(2,1)} %bitcast.359), calls=%async_computation.1 | async-start | bytes 3145728 | tf_op jit(solution)/shard_map/all_to_all | solution.py:30
  351.4 111.7 %all-reduce.3.cloned.1.call-done = bf16[2048,2,512]{2,1,0:T(2,128)(2,1)} async-done(((bf16[2048,2,512]{2,1,0:T(2,128)(2,1)}), bf16[2048,2,512]{2,1,0:T(2,128)(2,1)}) %all-reduce.3.cloned.1.call-update) | async-done | bytes 4194320
  (293 shorter events, 123.1 us)
Async XLA Ops:
  7.2 5.1 %copy-start.6 = (bf16[1,64,2,1792]{3,2,1,0:T(2,128)(2,1)S(1)}, bf16[1,64,2,1792]{3,2,1,0:T(2,128)(2,1)}, u32[]{:S(2)}) copy-start(bf16[1,64,2,1792]{3,2,1,0:T(2,128)(2,1)} %param.25) | copy-start | bytes 1376260
  7.2 6.2 %copy-start.10 = (s32[1,2]{1,0:T(1,128)S(1)}, s32[1,2]{1,0:T(1,128)}, u32[]{:S(2)}) copy-start(s32[1,2]{1,0:T(1,128)} %param.26) | copy-start | bytes 28
  7.2 78.0 %all-gather.3.cloned.1.call-start = ((), (), s32[]{:S(2)}) async-start(), calls=%async_computation.2 | async-start | bytes 3194880 | tf_op jit(solution)/shard_map/all_gather | solution.py:16
  8.7 123.2 %all-gather.5.cloned.1.call-start = ((), (), s32[]{:S(2)}) async-start(), calls=%async_computation.3 | async-start | bytes 4325376 | tf_op jit(solution)/shard_map/all_gather | solution.py:16
  88.4 3.5 copy-start.9
  111.5 28.3 %copy-start.3 = (bf16[6,512,2,128]{3,1,2,0:T(8,128)(2,1)}, bf16[6,512,2,128]{3,1,2,0:T(8,128)(2,1)S(1)}, u32[]{:S(2)}) copy-start(bf16[6,512,2,128]{3,1,2,0:T(8,128)(2,1)S(1)} %get-tuple-element.1289) | copy-start | bytes 4718596
  111.5 28.3 %copy-start.4 = (bf16[64,2,2,7,128]{4,0,3,1,2:T(8,128)(2,1)}, bf16[64,2,2,7,128]{4,0,3,1,2:T(8,128)(2,1)S(1)}, u32[]{:S(2)}) copy-start(bf16[64,2,2,7,128]{4,0,3,1,2:T(8,128)(2,1)S(1)} %get-tuple-element.1293) | copy-start | bytes 1376260
  221.5 10.5 %copy-start = (bf16[4,512,2,2,128]{4,1,3,2,0:T(8,128)(2,1)}, bf16[4,512,2,2,128]{4,1,3,2,0:T(8,128)(2,1)S(1)}, u32[]{:S(2)}) copy-start(bf16[4,512,2,2,128]{4,1,3,2,0:T(8,128)(2,1)S(1)} %get-tuple-element.1288) | copy-start | bytes 6291460
  232.0 3.1 copy-start.7
  241.3 3.1 copy-start.7
  250.6 3.2 copy-start.7
  259.9 3.1 copy-start.7
  269.2 3.1 copy-start.7
  278.5 3.1 copy-start.7
  287.8 5.6 %copy-start.2 = (f32[64,2,2,7,128]{4,0,3,1,2:T(8,128)}, f32[64,2,2,7,128]{4,0,3,1,2:T(8,128)S(1)}, u32[]{:S(2)}) copy-start(f32[64,2,2,7,128]{4,0,3,1,2:T(8,128)S(1)} %get-tuple-element.632) | copy-start | bytes 2752516
  287.8 6.9 %copy-start.1 = (bf16[4,512,2,2,128]{4,1,3,2,0:T(8,128)(2,1)S(1)}, bf16[4,512,2,2,128]{4,1,3,2,0:T(8,128)(2,1)}, u32[]{:S(2)}) copy-start(bf16[4,512,2,2,128]{4,1,3,2,0:T(8,128)(2,1)} %copy-done) | copy-start | bytes 6291460
  287.8 49.7 %all-to-all-start = ((bf16[2,1536,512]{2,1,0:T(8,128)(2,1)}), bf16[2,1536,512]{2,1,0:T(8,128)(2,1)}, u32[]{:S(2)}, u32[]{:S(2)}) async-start(bf16[2,1536,512]{2,1,0:T(8,128)(2,1)} %bitcast.360), calls=%async_computation | async-start | bytes 6291456 | tf_op jit(solution)/shard_map/all_to_all | solution.py:30
  293.4 169.7 %all-reduce.3.cloned.1.call-start = ((), (), s32[]{:S(2)}) async-start(), calls=%async_computation.4 | async-start | bytes 8388608
  294.7 2.0 copy-start.8
  302.6 2.0 copy-start.8
  310.5 2.0 copy-start.8
  318.4 2.0 copy-start.8
  337.4 9.5 %copy-start.11 = (u32[128]{0:T(128)S(1)}, u32[128]{0:T(128)}, u32[]{:S(2)}) copy-start(u32[128]{0:T(128)} %constant.116) | copy-start | bytes 1540
  337.4 10.7 %copy-start.5 = (bf16[64,2,2,7,128]{4,3,2,0,1:T(8,128)(2,1)S(1)}, bf16[64,2,2,7,128]{4,3,2,0,1:T(8,128)(2,1)}, u32[]{:S(2)}) copy-start(bf16[64,2,2,7,128]{4,3,2,0,1:T(8,128)(2,1)} %get-tuple-element.767) | copy-start | bytes 1376260
  341.6 123.1 %all-to-all-start.1 = ((bf16[32,48,512]{2,1,0:T(8,128)(2,1)}), bf16[32,48,512]{2,1,0:T(8,128)(2,1)S(1)}, u32[]{:S(2)}, u32[]{:S(2)}) async-start(bf16[32,48,512]{2,1,0:T(8,128)(2,1)} %bitcast.359), calls=%async_computation.1 | async-start | bytes 3145728 | tf_op jit(solution)/shard_map/all_to_all | solution.py:30
Sparse Core Ops, SparseCore 0:
  11.7 73.3 all-gather.2
  88.0 43.8 all-gather.4
  337.6 125.4 all-reduce.2
where the time goes:
time: 475 us; the launch traced here: 472 us
  waiting for transfers between devices  197 us (41%)
  matrix products  106 us (22%)
  local copies, waits for them, and re-layouts  89.4 us (19%)
  other arithmetic  52.6 us (11%)
  between operations  14.7 us (3%)
  starting transfers between devices  11 us (2%)
    unnamed x4, waiting for transfers between devices  112 us
    all_gather x2, waiting for transfers between devices, side_by_side(): lax.all_gather(both, axis, axis=dim, tiled=True)  85.4 us
    dot_general x10, matrix products, update(): jnp.einsum(forms[1], probs_low, value_block, preferred_element_type=jnp.f...  35.9 us
    dot_general x10, matrix products, update(): jnp.einsum(forms[0], douts, value_block, preferred_element_type=jnp.float32)  23 us
    dot_general x20, matrix products, scorer(): jnp.einsum(forms[0], query_view, key_block, preferred_element_type=jnp.fl...  20.7 us
    unnamed x38, local copies, waits for them, and re-layouts  19.4 us
    dynamic_slice x30, local copies, waits for them, and re-layouts, sweep_keys(): return lax.scan(advance, carried, (key_blocks, value_blocks, starts))  17.5 us
    dot_general x10, matrix products, update(): jnp.einsum(forms[1], grad_low, key_block, preferred_element_type=jnp.floa...  14.2 us
  transfers between devices with their start and end apart: 5, of which 3 were waited for; matrix products, arithmetic and copies ran while one was open for 19% of the time, Pallas kernels for 0%

commit v1 on v0

v1 whole, which is shorter than its diff:
```python
import functools

import jax
import jax.numpy as jnp
from jax import lax
from jax.experimental import pallas as pl
from jax.experimental.pallas import tpu as pltpu
from jax.sharding import PartitionSpec as P

HEAD_DIM = 128
RING = 4
CORES = 2
LOG2E = 1.4426950408889634
NEGATIVE = -1e30
MESH = pl.DeviceIdType.MESH
BF16 = jnp.bfloat16
F32 = jnp.float32


def place():
    s = lax.axis_index("seq")
    return s // (RING * CORES), (s // CORES) % RING, s % CORES


def seq_of(h, p, q, core):
    z, y = (q, p) if h == 0 else (p, q)
    return (z * RING + y) * CORES + core


def grid_at(ref, h, p, q, core):
    if h == 0:
        return ref.at[h, q, p, core]
    return ref.at[h, p, q, core]


def greet():
    z, y, core = place()
    pair = lax.axis_index("pair")
    barrier = pltpu.get_barrier_semaphore()
    peers = []
    for h in range(2):
        p, q = (y, z) if h == 0 else (z, y)
        for d in (1, RING - 1):
            peers.append({"seq": seq_of(h, (p + d) % RING, q, core)})
    peers.append({"seq": seq_of(0, y, z, 1 - core)})
    peers.append({"pair": 1 - pair})
    for peer in peers:
        pl.semaphore_signal(barrier, inc=1, device_id=peer, device_id_type=MESH)
    pl.semaphore_wait(barrier, len(peers))


class Copies:
    def __init__(self, send_sem, recv_sem):
        self.send_sem, self.recv_sem = send_sem, recv_sem
        self.ids = {}
        self.sent = []

    def make(self, key, src, dst, to):
        n = self.ids.setdefault(key, len(self.ids))
        return pltpu.make_async_remote_copy(
            src_ref=src,
            dst_ref=dst,
            send_sem=self.send_sem.at[n],
            recv_sem=self.recv_sem.at[n],
            device_id=to,
            device_id_type=MESH,
        )

    def send(self, key, src, dst, to):
        copy = self.make(key, src, dst, to)
        copy.start()
        self.sent.append(copy)

    def arrived(self, key, dst, to):
        self.make(key, dst, dst, to).wait_recv()

    def finish(self):
        for copy in self.sent:
            copy.wait_send()


GATHER_COPIES = 120
ORDER = (0, 3, 1, 2)


def gather_kernel(ans_rows, pre_rows, ans_ref, pre_ref, out_ref, held, send_sem, recv_sem, local_sem, out_sem):
    z, y, core = place()
    pair = lax.axis_index("pair")
    rows = ans_rows + 2 * pre_rows
    half = rows // 2
    parts = (pl.ds(0, half), pl.ds(half, rows - half))
    pieces = (pl.ds(0, ans_rows), pl.ds(ans_rows, 2 * pre_rows))
    whole = pl.ds(0, rows)
    mine = pl.ds(pl.multiple_of(ans_rows + pair * pre_rows, 16), pre_rows)
    other = pl.ds(pl.multiple_of(ans_rows + (1 - pair) * pre_rows, 16), pre_rows)
    at = ((y, z), (z, y))
    copies = Copies(send_sem, recv_sem)
    stores = []

    def block(h, p, q, part):
        return held.at[h, p, q, part]

    def to(h, dp, dq):
        p, q = at[h]
        return {"seq": seq_of(h, (p + dp) % RING, (q + dq) % RING, core)}

    sibling = {"seq": seq_of(0, y, z, 1 - core)}

    locals_ = []
    for h in range(2):
        p, q = at[h]
        locals_.append(pltpu.make_async_copy(ans_ref.at[h], block(h, p, q, pieces[0]), local_sem.at[2 * h]))
        locals_.append(pltpu.make_async_copy(pre_ref.at[h], block(h, p, q, mine), local_sem.at[2 * h + 1]))
    for copy in locals_:
        copy.start()
    greet()
    for h in range(2):
        p, q = at[h]
        copies.send(("pair", h), pre_ref.at[h], block(h, p, q, mine), {"pair": 1 - pair})

    def forward(h, k, axis, p, q, source, part, direction, key):
        dp, dq = (direction, 0) if axis == 0 else (0, direction)
        ref = block(h, p, q, part)
        copies.send(key, ref, ref, to(h, dp, dq))

    def own_first(piece):
        for h in range(2):
            p, q = at[h]
            for direction in (1, 3):
                forward(h, 0, 0, p, q, None, pieces[piece], direction, ("one", h, direction, piece))
        for h in range(2):
            p, q = at[h]
            for direction in (1, 3):
                forward(h, 0, 1, p, q, None, pieces[piece], direction, ("two", h, 0, direction, piece))

    def spread(h, k):
        p, q = at[h]
        source = (p + ORDER[k]) % RING
        for direction in (1, 3):
            forward(h, k, 1, source, q, None, whole, direction, ("two", h, k, direction, 2))

    def share(h, p, q, key):
        ref = block(h, p, q, whole)
        copies.send(("sib", h, key), ref, grid_at(out_ref, h, p, q, core), sibling)
        n = len(stores)
        store = pltpu.make_async_copy(ref, grid_at(out_ref, h, p, q, core), out_sem.at[n])
        store.start()
        stores.append(store)

    locals_[0].wait()
    locals_[2].wait()
    own_first(0)
    locals_[1].wait()
    locals_[3].wait()
    for h in range(2):
        p, q = at[h]
        copies.arrived(("pair", h), block(h, p, q, other), {"pair": 1 - pair})
    own_first(1)
    for h in range(2):
        p, q = at[h]
        share(h, p, q, (0, 0))

    for direction in (1, 3):
        for h in range(2):
            p, q = at[h]
            source = (p - direction) % RING
            for piece in range(2):
                copies.arrived(("one", h, direction, piece), block(h, source, q, pieces[piece]), to(h, direction, 0))
            forward(h, 0, 0, source, q, None, parts[direction // 2], direction, ("far", h, direction))
            spread(h, ORDER.index((-direction) % RING))
            share(h, source, q, ((-direction) % RING, 0))
    for h in range(2):
        p, q = at[h]
        source = (p + 2) % RING
        for direction in (1, 3):
            copies.arrived(("far", h, direction), block(h, source, q, parts[direction // 2]), to(h, direction, 0))
        spread(h, 3)
        share(h, source, q, (2, 0))
    for k in range(RING):
        for direction in (1, 3):
            for h in range(2):
                p, q = at[h]
                p_source, q_source = (p + ORDER[k]) % RING, (q - direction) % RING
                for piece in (range(2) if k == 0 else (2,)):
                    area = whole if piece == 2 else pieces[piece]
                    copies.arrived(("two", h, k, direction, piece), block(h, p_source, q_source, area), to(h, 0, direction))
                forward(h, k, 1, p_source, q_source, None, parts[direction // 2], direction, ("far2", h, k, direction))
                share(h, p_source, q_source, (ORDER[k], (-direction) % RING))
    for k in range(RING):
        for h in range(2):
            p, q = at[h]
            p_source, q_source = (p + ORDER[k]) % RING, (q + 2) % RING
            for direction in (1, 3):
                copies.arrived(("far2", h, k, direction), block(h, p_source, q_source, parts[direction // 2]), to(h, 0, direction))
            share(h, p_source, q_source, (ORDER[k], 2))
    for h in range(2):
        p, q = at[h]
        for dp in range(RING):
            for dq in range(RING):
                area = grid_at(out_ref, h, (p + dp) % RING, (q + dq) % RING, 1 - core)
                copies.arrived(("sib", h, (dp, dq)), area, sibling)
    for store in stores:
        store.wait()
    copies.finish()


def gather(ans, pre):
    kv, ans_rows, width = ans.shape
    pre_rows = pre.shape[1]
    rows = ans_rows + 2 * pre_rows
    return pl.pallas_call(
        functools.partial(gather_kernel, ans_rows, pre_rows),
        out_shape=jax.ShapeDtypeStruct((kv, RING, RING, CORES, rows, width), ans.dtype),
        in_specs=[pl.BlockSpec(memory_space=pltpu.VMEM)] * 2,
        out_specs=pl.BlockSpec(memory_space=pl.ANY),
        scratch_shapes=[
            pltpu.VMEM((kv, RING, RING, rows, width), ans.dtype),
            pltpu.SemaphoreType.DMA((GATHER_COPIES,)),
            pltpu.SemaphoreType.DMA((GATHER_COPIES,)),
            pltpu.SemaphoreType.DMA((4,)),
            pltpu.SemaphoreType.DMA((32,)),
        ],
        compiler_params=pltpu.CompilerParams(collective_id=0, has_side_effects=True),
        name="gather",
    )(ans, pre)


SCATTER_COPIES = 60


def scatter_kernel(
    ans_rows, pre_rows, terms_ref, ans_out, pre_out, total, beside, far2, near2, far1, near1, swap, send_sem, recv_sem, local_sem
):
    z, y, core = place()
    pair = lax.axis_index("pair")
    rows = ans_rows + 2 * pre_rows
    half = rows // 2
    parts = (pl.ds(0, half), pl.ds(half, rows - half))
    mine = pl.ds(pl.multiple_of(ans_rows + pair * pre_rows, 16), pre_rows)
    other = pl.ds(pl.multiple_of(ans_rows + (1 - pair) * pre_rows, 16), pre_rows)
    at = ((y, z), (z, y))
    copies = Copies(send_sem, recv_sem)
    sibling = {"seq": seq_of(0, y, z, 1 - core)}

    def to(h, dp, dq):
        p, q = at[h]
        return {"seq": seq_of(h, (p + dp) % RING, (q + dq) % RING, core)}

    def column(h, p, c):
        if h == 0:
            return terms_ref.at[h, :, p, c]
        return terms_ref.at[h, p, :, c]

    order = (2, 1, 3, 0)
    loads = {}
    for k in range(RING):
        for h in range(2):
            p = (at[h][0] + order[k]) % RING
            loads[h, k] = pltpu.make_async_copy(column(h, p, core), total.at[h, p], local_sem.at[h * RING + k])
            loads[h, k].start()
    greet()
    for k in range(RING):
        for h in range(2):
            p = (at[h][0] + order[k]) % RING
            copies.send(("sib", h, k), column(h, p, 1 - core), beside.at[h, p], sibling)

    def add(into, other_ref):
        into[...] = (into[...].astype(F32) + other_ref[...].astype(F32)).astype(BF16)

    for k in range(RING):
        for h in range(2):
            p, q = at[h]
            target = (p + order[k]) % RING
            loads[h, k].wait()
            copies.arrived(("sib", h, k), beside.at[h, target], sibling)
            far = (q + 2) % RING
            add(total.at[h, target, far], beside.at[h, target, far])
            for n, direction in enumerate((1, 3)):
                copies.send(
                    ("far2", h, k, n), total.at[h, target, far, parts[n]], far2.at[h, k, n], to(h, 0, direction)
                )
            for d in (1, 3, 0):
                place_q = (q + d) % RING
                add(total.at[h, target, place_q], beside.at[h, target, place_q])
    for k in range(RING):
        for h in range(2):
            p, q = at[h]
            target = (p + order[k]) % RING
            for n, direction in enumerate((1, 3)):
                nearby = (q + direction) % RING
                copies.arrived(("far2", h, k, n), far2.at[h, k, n], to(h, 0, direction))
                add(total.at[h, target, nearby, parts[n]], far2.at[h, k, n])
                copies.send(("near2", h, k, n), total.at[h, target, nearby], near2.at[h, k, n], to(h, 0, direction))

    def settle2(h, k):
        p, q = at[h]
        target = (p + order[k]) % RING
        for n, direction in enumerate((1, 3)):
            copies.arrived(("near2", h, k, n), near2.at[h, k, n], to(h, 0, direction))
        into = total.at[h, target, q]
        into[...] = (
            into[...].astype(F32) + near2[h, k, 0].astype(F32) + near2[h, k, 1].astype(F32)
        ).astype(BF16)

    for h in range(2):
        p, q = at[h]
        settle2(h, 0)
        for n, direction in enumerate((1, 3)):
            copies.send(("far1", h, n), total.at[h, (p + 2) % RING, q, parts[n]], far1.at[h, n], to(h, direction, 0))
    for k in (1, 2):
        n = k - 1
        direction = order[k]
        for h in range(2):
            p, q = at[h]
            settle2(h, k)
            nearby = (p + direction) % RING
            copies.arrived(("far1", h, n), far1.at[h, n], to(h, direction, 0))
            add(total.at[h, nearby, q, parts[n]], far1.at[h, n])
            copies.send(("near1", h, n), total.at[h, nearby, q], near1.at[h, n], to(h, direction, 0))
    for h in range(2):
        settle2(h, 3)
    for h in range(2):
        p, q = at[h]
        for n, direction in enumerate((1, 3)):
            copies.arrived(("near1", h, n), near1.at[h, n], to(h, direction, 0))
        into = total.at[h, p, q]

        def final(area):
            return (
                total[h, p, q, area].astype(F32) + near1[h, 0, area].astype(F32) + near1[h, 1, area].astype(F32)
            )

        swap[0, h] = final(other).astype(BF16)
        copies.send(("swap", h), swap.at[0, h], swap.at[1, h], {"pair": 1 - pair})
        pre_out[h] = final(mine)
        ans_out[h] = final(pl.ds(0, ans_rows)).astype(BF16)
    for h in range(2):
        copies.arrived(("swap", h), swap.at[1, h], {"pair": 1 - pair})
        pre_out[h] = pre_out[h] + swap[1, h].astype(F32)
    copies.finish()


def scatter(terms, ans_rows, pre_rows):
    kv, _, _, _, rows, width = terms.shape
    half = rows // 2
    return pl.pallas_call(
        functools.partial(scatter_kernel, ans_rows, pre_rows),
        out_shape=(
            jax.ShapeDtypeStruct((kv, ans_rows, width), BF16),
            jax.ShapeDtypeStruct((kv, pre_rows, width), F32),
        ),
        in_specs=[pl.BlockSpec(memory_space=pl.ANY)],
        out_specs=(pl.BlockSpec(memory_space=pltpu.VMEM), pl.BlockSpec(memory_space=pltpu.VMEM)),
        scratch_shapes=[
            pltpu.VMEM((kv, RING, RING, rows, width), BF16),
            pltpu.VMEM((kv, RING, RING, rows, width), BF16),
            pltpu.VMEM((kv, RING, 2, half, width), BF16),
            pltpu.VMEM((kv, RING, 2, rows, width), BF16),
            pltpu.VMEM((kv, 2, half, width), BF16),
            pltpu.VMEM((kv, 2, rows, width), BF16),
            pltpu.VMEM((2, kv, pre_rows, width), BF16),
            pltpu.SemaphoreType.DMA((SCATTER_COPIES,)),
            pltpu.SemaphoreType.DMA((SCATTER_COPIES,)),
            pltpu.SemaphoreType.DMA((2 * RING,)),
        ],
        compiler_params=pltpu.CompilerParams(collective_id=1, has_side_effects=True),
        name="scatter",
    )(terms)


def nn(a, b):
    return lax.dot_general(a, b, (((1,), (0,)), ((), ())), preferred_element_type=F32)


def nt(a, b):
    return lax.dot_general(a, b, (((1,), (1,)), ((), ())), preferred_element_type=F32)


ANS_SOURCES = 4
PRE_SOURCES = 8


def attend_kernel(
    ans_here,
    pre_rows,
    group,
    length_ref,
    limit_ref,
    q_ref,
    g_ref,
    kv_ref,
    out_ref,
    dq_ref,
    terms_ref,
    scores,
    weights,
    queries,
    douts,
    queries_t,
    douts_t,
    prefix_terms,
    top,
    row_sum,
    acc_t,
):
    sources = kv_ref.shape[1]
    d = HEAD_DIM
    b = pl.program_id(1)
    s = lax.axis_index("seq")
    scale = d**-0.5
    rows = group * ans_here
    ans_chunk = ANS_SOURCES * ans_here
    pre_chunk = PRE_SOURCES * pre_rows
    per_pair = sources // PRE_SOURCES
    pre_total = 2 * sources * pre_rows
    first_row = s * ans_here
    length = length_ref[0, b]
    limit = limit_ref[0, b]
    ans_at = pl.multiple_of(b * ans_here, ans_here)
    live_here = first_row < length
    n_pre = jnp.where(live_here, (limit + pre_chunk - 1) // pre_chunk, 0)
    n_full = jnp.where(live_here, limit // pre_chunk, 0)
    n_ans = jnp.where(live_here, s // ANS_SOURCES + 1, 0)

    @pl.when(b == 0)
    def _():
        prefix_terms[...] = jnp.zeros_like(prefix_terms)

    terms_ref[0, :, pl.ds(ans_at, ans_here), :] = jnp.zeros((sources, ans_here, 2 * d), BF16)

    def pre_block(i, lanes):
        pair_at, source = i // per_pair, (i % per_pair) * PRE_SOURCES
        row = pl.multiple_of(2 * ans_here + pair_at * pre_rows, 16)
        part = kv_ref[0, pl.ds(source, PRE_SOURCES), pl.ds(row, pre_rows), lanes]
        return part.reshape(pre_chunk, d)

    def ans_block(i, lanes):
        part = kv_ref[0, pl.ds(i * ANS_SOURCES, ANS_SOURCES), pl.ds(ans_at, ans_here), lanes]
        return part.reshape(ans_chunk, d)

    keys_at, values_at = slice(0, d), slice(d, 2 * d)

    def pre_span(i):
        return pl.ds(pl.multiple_of(i * pre_chunk, pre_chunk), pre_chunk)

    def ans_span(i):
        return pl.ds(pl.multiple_of(pre_total + i * ans_chunk, ans_chunk), ans_chunk)

    def fold(values, into):
        return jnp.maximum(into, jnp.max(values.reshape(values.shape[0] // 8, 8, rows), axis=0))

    @pl.when(live_here)
    def _():
        place_rows = lax.broadcasted_iota(jnp.int32, (ans_here, d), 0)
        alive = place_rows + first_row < length
        for g in range(group):
            lanes = slice(g * d, (g + 1) * d)
            here = slice(g * ans_here, (g + 1) * ans_here)
            queries[here] = q_ref[0, :, lanes]
            douts[here] = jnp.where(alive, g_ref[0, :, lanes].astype(F32), 0.0)
        douts_t[...] = douts[...].T
        top[...] = jnp.full_like(top, NEGATIVE)

        def score(i, block, span, keep):
            values = nt(block(i, keys_at), queries[...])
            if keep is not None:
                values = jnp.where(keep(i, values.shape), values, NEGATIVE)
            scores[span(i)] = values
            top[...] = fold(values, top[...])

        def pre_keep(i, shape):
            return lax.broadcasted_iota(jnp.int32, shape, 0) + i * pre_chunk < limit

        def ans_keep(i, shape):
            key = lax.broadcasted_iota(jnp.int32, shape, 0) + i * ans_chunk
            row = lax.broadcasted_iota(jnp.int32, shape, 1) % ans_here + first_row
            return key <= row

        @pl.loop(0, n_full)
        def _(i):
            score(i, pre_block, pre_span, None)

        @pl.when(n_full < n_pre)
        def _():
            score(n_full, pre_block, pre_span, pre_keep)

        @pl.loop(0, n_ans - 1)
        def _(i):
            score(i, ans_block, ans_span, None)

        score(n_ans - 1, ans_block, ans_span, ans_keep)

        top_row = jnp.max(top[...], axis=0, keepdims=True)
        shift = top_row * (scale * LOG2E)
        row_sum[...] = jnp.zeros_like(row_sum)
        acc_t[...] = jnp.zeros_like(acc_t)

        def spread(i, block, span):
            e = jnp.exp2(scores[span(i)] * (scale * LOG2E) - shift)
            row_sum[...] += jnp.sum(e.reshape(e.shape[0] // 8, 8, rows), axis=0)
            low = e.astype(BF16)
            weights[span(i)] = low
            acc_t[...] += nn(block(i, values_at).T, low)

        @pl.loop(0, n_pre)
        def _(i):
            spread(i, pre_block, pre_span)

        @pl.loop(0, n_ans)
        def _(i):
            spread(i, ans_block, ans_span)

        inverse = 1.0 / jnp.sum(row_sum[...], axis=0, keepdims=True)
        attended_t = acc_t[...] * inverse
        scaled = (douts_t[...] * inverse).astype(BF16)
        delta = jnp.sum(scaled.astype(F32) * attended_t, axis=0, keepdims=True)
        douts_low_t = scaled
        queries_t[...] = douts_low_t
        douts_low = douts_low_t.astype(F32).T.astype(BF16)
        attended = attended_t.T
        for g in range(group):
            lanes = slice(g * d, (g + 1) * d)
            here = slice(g * ans_here, (g + 1) * ans_here)
            out_ref[0, :, lanes] = jnp.where(alive, attended[here], 0.0).astype(BF16)
        douts[...] = douts_low.astype(F32)
        acc_t[...] = jnp.zeros_like(acc_t)

        def back(i, block, span):
            low = weights[span(i)]
            grad_probs = nn(block(i, values_at), queries_t[...])
            grad_low = (low.astype(F32) * (grad_probs - delta)).astype(BF16)
            value_term = nn(low, douts_low)
            key_term = nn(grad_low, queries[...]) * scale
            acc_t[...] += nn(block(i, keys_at).T, grad_low)
            return key_term, value_term

        @pl.loop(0, n_pre)
        def _(i):
            key_term, value_term = back(i, pre_block, pre_span)
            prefix_terms[pre_span(i), 0:d] += key_term
            prefix_terms[pre_span(i), d : 2 * d] += value_term

        @pl.loop(0, n_ans)
        def _(i):
            key_term, value_term = back(i, ans_block, ans_span)
            at = pl.ds(i * ANS_SOURCES, ANS_SOURCES)
            span = pl.ds(ans_at, ans_here)
            terms_ref[0, at, span, 0:d] = key_term.astype(BF16).reshape(ANS_SOURCES, ans_here, d)
            terms_ref[0, at, span, d : 2 * d] = value_term.astype(BF16).reshape(ANS_SOURCES, ans_here, d)

        grad_queries = (acc_t[...] * scale).T
        for g in range(group):
            lanes = slice(g * d, (g + 1) * d)
            here = slice(g * ans_here, (g + 1) * ans_here)
            dq_ref[0, :, lanes] = grad_queries[here].astype(BF16)

    @pl.when(jnp.logical_not(live_here))
    def _():
        out_ref[...] = jnp.zeros_like(out_ref)
        dq_ref[...] = jnp.zeros_like(dq_ref)

    @pl.when(b == 1)
    def _():
        @pl.loop(0, 2 * per_pair)
        def _(i):
            pair_at, source = i // per_pair, (i % per_pair) * PRE_SOURCES
            row = pl.multiple_of(2 * ans_here + pair_at * pre_rows, 16)
            terms_ref[0, pl.ds(source, PRE_SOURCES), pl.ds(row, pre_rows), :] = (
                prefix_terms[pre_span(i)].astype(BF16).reshape(PRE_SOURCES, pre_rows, 2 * d)
            )


def attend(queries, grad_out, gathered, lengths, limits, ans_here, pre_rows):
    batch, _, features = queries.shape
    kv, sources, rows_all, width = gathered.shape
    d = HEAD_DIM
    group = features // d // kv
    keys_total = sources * ans_here + 2 * sources * pre_rows
    rows = group * ans_here
    query_spec = pl.BlockSpec((1, ans_here, group * d), lambda c, b: (b, 0, c))
    kv_spec = pl.BlockSpec((1, sources, rows_all, width), lambda c, b: (c, 0, 0, 0))
    smem = pl.BlockSpec(memory_space=pltpu.SMEM)
    return pl.pallas_call(
        functools.partial(attend_kernel, ans_here, pre_rows, group),
        grid=(kv, batch),
        out_shape=(
            jax.ShapeDtypeStruct(queries.shape, BF16),
            jax.ShapeDtypeStruct(queries.shape, BF16),
            jax.ShapeDtypeStruct(gathered.shape, BF16),
        ),
        in_specs=[smem, smem, query_spec, query_spec, kv_spec],
        out_specs=(query_spec, query_spec, kv_spec),
        scratch_shapes=[
            pltpu.VMEM((keys_total, rows), F32),
            pltpu.VMEM((keys_total, rows), BF16),
            pltpu.VMEM((rows, d), BF16),
            pltpu.VMEM((rows, d), F32),
            pltpu.VMEM((d, rows), BF16),
            pltpu.VMEM((d, rows), F32),
            pltpu.VMEM((2 * sources * pre_rows, width), F32),
            pltpu.VMEM((8, rows), F32),
            pltpu.VMEM((8, rows), F32),
            pltpu.VMEM((d, rows), F32),
        ],
        compiler_params=pltpu.CompilerParams(
            dimension_semantics=("arbitrary", "arbitrary"), vmem_limit_bytes=60 * 1024 * 1024
        ),
        name="attend",
    )(lengths, limits, queries, grad_out, gathered)


def on_device(
    queries,
    answer_keys,
    answer_values,
    prefix_keys,
    prefix_values,
    grad_out,
    answer_length,
    prefix_limit,
):
    d = HEAD_DIM
    _, ans_here, batch, features = queries.shape
    kv = answer_keys.shape[3] // d
    pre_rows = prefix_keys.shape[0]
    side = lax.axis_size("seq")

    def by_head(keys, values):
        both = jnp.stack([keys.reshape(-1, kv, d), values.reshape(-1, kv, d)], axis=2)
        return both.transpose(1, 0, 2, 3).reshape(kv, -1, 2 * d)

    def batch_first(x):
        return x[0].transpose(1, 0, 2)

    ans = by_head(batch_first(answer_keys), batch_first(answer_values))
    pre = by_head(prefix_keys, prefix_values)
    gathered = gather(ans, pre)
    flat = gathered.reshape(kv, side, gathered.shape[-2], 2 * d)
    out, grad_queries, terms = attend(
        batch_first(queries), batch_first(grad_out), flat, answer_length, prefix_limit, ans_here, pre_rows
    )
    ans_sums, pre_sums = scatter(terms.reshape(gathered.shape), batch * ans_here, pre_rows)

    def back(x):
        return x.transpose(1, 0, 2)[None]

    def apart(x, n):
        return x[:, :, n * d : (n + 1) * d]

    def ans_grad(n):
        x = apart(ans_sums, n).reshape(kv, batch, ans_here, d).transpose(2, 1, 0, 3)
        return x.reshape(answer_keys.shape)

    def pre_grad(n):
        return apart(pre_sums, n).transpose(1, 0, 2).reshape(prefix_keys.shape)

    return (back(out), back(grad_queries), ans_grad(0), ans_grad(1), pre_grad(0), pre_grad(1))


def solution(mesh):
    tokens = P("pair", "seq", None, "head")
    prefix = P(("pair", "seq"), "head")
    scalars = P("pair", None)
    return jax.shard_map(
        on_device,
        mesh=mesh,
        in_specs=(tokens, tokens, tokens, prefix, prefix, tokens, scalars, scalars),
        out_specs=(tokens, tokens, tokens, tokens, prefix, prefix),
        check_vma=False,
    )
```

time: 475 us -> 134 us (0.28)
  waiting for transfers between devices: 197 us -> 0 us
  Pallas kernels: 0 us -> 117 us
  matrix products: 106 us -> 0 us
  local copies, waits for them, and re-layouts: 89.4 us -> 16 us
  other arithmetic: 52.6 us -> 0.3 us
  between operations: 14.7 us -> 0.72 us
  starting transfers between devices: 11 us -> 0 us
    pallas_call x0 -> x3, Pallas kernels: none -> 117 us  [the longest x1 50.4 us: scatter(): pl.pallas_call(functools.partial(scatter_kernel, ans_rows, pre_rows), out...]
    unnamed x4 -> x0, waiting for transfers between devices: 112 us -> none
    dot_general x70 -> x0, matrix products: 106 us -> none  [the longest x10 35.9 us: update(): jnp.einsum(forms[1], probs_low, value_block, preferred_element_type=jnp.f...]
    all_gather x2 -> x0, waiting for transfers between devices: 85.4 us -> none  [side_by_side(): lax.all_gather(both, axis, axis=dim, tiled=True)]
    reduce_sum x13 -> x0, other arithmetic: 19.8 us -> none  [the longest x10 11.9 us: update(): jnp.sum(jnp.where(allowed, jnp.exp(masked - new_top[..., None]), 0.0), ax...]
    add x54 -> x0, other arithmetic: 19.6 us -> none  [the longest x18 11.6 us: prefix_allowed_keys(): places = first + lax.iota(jnp.int32, key_span)]
    another operation x6, local copies, waits for them, and re-layouts: 20.9 us -> 1.63 us  [by_head(): jnp.stack([keys.reshape(-1, kv, d), values.reshape(-1, kv, d)], axis=2)]
    dynamic_slice x30 -> x0, local copies, waits for them, and re-layouts: 17.5 us -> none  [sweep_keys(): return lax.scan(advance, carried, (key_blocks, value_blocks, starts))]
  transfers between devices with their start and end apart: 5 -> 0, of which waited for: 3 -> 0; matrix products, arithmetic and copies ran while one was open for 19% -> 0% of each run, Pallas kernels for 0% -> 0%
where the time goes in v1:
time: 134 us
  Pallas kernels  117 us (87%)
  local copies, waits for them, and re-layouts  16 us (12%)
    pallas_call x1, Pallas kernels, scatter(): pl.pallas_call(functools.partial(scatter_kernel, ans_rows, pre_rows), out...  50.4 us
    pallas_call x1, Pallas kernels, gather(): pl.pallas_call(functools.partial(gather_kernel, ans_rows, pre_rows), out_...  35.8 us
    pallas_call x1, Pallas kernels, attend(): pl.pallas_call(functools.partial(attend_kernel, ans_here, pre_rows, group...  31.3 us
    unnamed x3, local copies, waits for them, and re-layouts  5.34 us
    transpose x3, local copies, waits for them, and re-layouts, batch_first(): return x[0].transpose(1, 0, 2)  3.86 us

profile of v1, /device:TPU:1, one launch (start us, length us, event | category | flops | bytes accessed | tf_op | source)
XLA Modules:
  0.0 134.4 jit_solution(14804138020577410330)
XLA Ops:
  0.6 0.8 stack_reshape.14
  1.4 0.8 stack_reshape.15
  2.2 0.1 maximum_bitcast_fusion.1
  2.4 0.7 reshape.43.pre_ref
  3.0 0.8 copy.24
  3.9 0.9 copy.25
  4.8 0.2 maximum_bitcast_fusion
  5.0 0.1 copy.26
  5.1 0.7 reshape.42.ans_ref
  5.8 2.2 %copy_bitcast_fusion = (bf16[2,64,1792]{2,1,0:T(8,128)(2,1)}, bf16[2,64,1792]{2,1,0:T(8,128)(2,1)}) fusion(bf16[1,64,2,1792]{3,2,1,0:T(2,128)(2,1)} %param.13, bf16[1,64,2,1792]{3,2,1,0:T(2,128)(2,1)} %param.8), kind=kLoop, calls=%fused_computation | loop fusion | bytes 1835008 | tf_op jit(solution)/shard_map/transpose | solution.py:633
  8.0 35.8 %gather.1 = bf16[2,4,4,2,224,256]{5,4,3,2,1,0:T(8,128)(2,1)} custom-call(bf16[2,128,256]{2,1,0:T(8,128)(2,1)} %reshape.42.ans_ref, bf16[2,48,256]{2,1,0:T(8,128)(2,1)} %reshape.43.pre_ref), custom_call_target="tpu_custom_call" | custom-call | tf_op jit(solution)/shard_map/gather/pallas_call | solution.py:211
  43.8 31.3 %attend.1 = (bf16[2,64,1792]{2,1,0:T(8,128)(2,1)}, bf16[2,64,1792]{2,1,0:T(8,128)(2,1)}, bf16[2,32,224,256]{3,2,1,0:T(8,128)(2,1)}) custom-call(s32[1,2]{1,0:T(1,128)} %length_ref.1, s32[1,2]{1,0:T(1,128)} %limit_ref.1, bf16[2,64,1792]{2,1,0:T(8,128)(2,1)} %get-tuple-element.33.q_ref, bf16[2,64,1792]{2,1,0:T(8,128)(2,1)} %get-tuple-element.32.g_ref, ...), custom_call_target="tpu_custom_call" | custom-call | tf_op jit(solution)/shard_map/attend/pallas_call | solution.py:583
  75.0 2.3 %copy.33 = bf16[1,64,2,1792]{3,2,1,0:T(2,128)(2,1)} copy(bf16[1,64,2,1792]{3,1,2,0:T(8,128)(2,1)} %bitcast.47) | data formatting | bytes 917504
  77.3 2.3 %copy.34 = bf16[1,64,2,1792]{3,2,1,0:T(2,128)(2,1)} copy(bf16[1,64,2,1792]{3,1,2,0:T(8,128)(2,1)} %bitcast.46) | data formatting | bytes 917504
  79.5 50.4 %scatter.1 = (bf16[2,128,256]{2,1,0:T(8,128)(2,1)}, f32[2,48,256]{2,1,0:T(8,128)}) custom-call(bf16[2,4,4,2,224,256]{5,4,3,2,1,0:T(8,128)(2,1)} %bitcast.45), custom_call_target="tpu_custom_call" | custom-call | tf_op jit(solution)/shard_map/scatter/pallas_call | solution.py:346
  130.0 0.9 fusion
  130.8 0.1 copy.30
  130.9 0.7 reshape.49
  131.6 0.1 copy.29
  131.7 0.7 reshape.47
  132.4 0.8 slice_bitcast_fusion
  133.2 0.6 copy.41
  133.8 0.6 copy.42
  (4 shorter events, 0.1 us)

commit v2 on v1

v2 whole, which is shorter than its diff:
```python
import functools

import jax
import jax.numpy as jnp
from jax import lax
from jax.experimental import pallas as pl
from jax.experimental.pallas import tpu as pltpu
from jax.sharding import PartitionSpec as P

HEAD_DIM = 128
RING = 4
CORES = 2
LOG2E = 1.4426950408889634
NEGATIVE = -1e30
MESH = pl.DeviceIdType.MESH
BF16 = jnp.bfloat16
F32 = jnp.float32


def place():
    s = lax.axis_index("seq")
    return s // (RING * CORES), (s // CORES) % RING, s % CORES


def seq_of(z, y, core):
    return (z * RING + y) * CORES + core


def shifted(h, dp, dq):
    z, y, _ = place()
    return (z + dp * h + dq * (1 - h)) % RING, (y + dp * (1 - h) + dq * h) % RING


def to(h, dp, dq):
    z, y = shifted(h, dp, dq)
    return {"seq": seq_of(z, y, place()[2])}


def across(same_core):
    z, y, core = place()
    target = {"pair": 1 - lax.axis_index("pair")}
    if not same_core:
        target["seq"] = seq_of(z, y, 1 - core)
    return target


def sibling():
    z, y, core = place()
    return {"seq": seq_of(z, y, 1 - core)}


def greet():
    barrier = pltpu.get_barrier_semaphore()
    peers = [to(h, d, 0) for h in range(2) for d in (1, RING - 1)]
    peers += [sibling(), across(True), across(False)]
    for peer in peers:
        pl.semaphore_signal(barrier, inc=1, device_id=peer, device_id_type=MESH)
    pl.semaphore_wait(barrier, len(peers))


def spans(ans_rows, pre_rows):
    pair = lax.axis_index("pair")
    rows = ans_rows + 2 * pre_rows
    half = rows // 2
    parts = (pl.ds(0, half), pl.ds(half, rows - half))
    mine = pl.ds(pl.multiple_of(ans_rows + pair * pre_rows, 16), pre_rows)
    other = pl.ds(pl.multiple_of(ans_rows + (1 - pair) * pre_rows, 16), pre_rows)
    return rows, parts, mine, other


class Copies:
    def __init__(self, send_sem, recv_sem):
        self.send_sem, self.recv_sem = send_sem, recv_sem
        self.ids = {}
        self.sent = []

    def make(self, key, src, dst, to):
        n = self.ids.setdefault(key, len(self.ids))
        return pltpu.make_async_remote_copy(
            src_ref=src,
            dst_ref=dst,
            send_sem=self.send_sem.at[n],
            recv_sem=self.recv_sem.at[n],
            device_id=to,
            device_id_type=MESH,
        )

    def send(self, key, src, dst, to):
        copy = self.make(key, src, dst, to)
        copy.start()
        self.sent.append(copy)

    def arrived(self, key, dst, to):
        self.make(key, dst, dst, to).wait_recv()

    def finish(self):
        for copy in self.sent:
            copy.wait_send()


ORDER = (0, 3, 1, 2)
GATHER_COPIES = 80


def gather_kernel(
    ans_rows, pre_rows, ans_ref, pre_ref, q_ref, g_ref, kv_out, q_out, g_out, held, send_sem, recv_sem, local_sem, out_sem
):
    z, y, core = place()
    rows, parts, mine, other = spans(ans_rows, pre_rows)
    pieces = (pl.ds(0, ans_rows), pl.ds(ans_rows, 2 * pre_rows))
    copies = Copies(send_sem, recv_sem)
    sources = (core, 1 - core)
    stores = []

    def block(r, dp, dq):
        zz, yy = shifted(sources[r], dp, dq)
        return held.at[zz, yy, sources[r]]

    pos = q_ref.shape[2]
    own_rows = pl.ds(pl.multiple_of(core * pos, pos), pos)
    sibling_rows = pl.ds(pl.multiple_of((1 - core) * pos, pos), pos)
    loads = [
        pltpu.make_async_copy(ans_ref.at[core], block(0, 0, 0).at[pieces[0]], local_sem.at[0]),
        pltpu.make_async_copy(pre_ref.at[core], block(0, 0, 0).at[mine], local_sem.at[1]),
        pltpu.make_async_copy(q_ref.at[core], q_out.at[:, own_rows], local_sem.at[2]),
        pltpu.make_async_copy(g_ref.at[core], g_out.at[:, own_rows], local_sem.at[3]),
    ]
    for copy in loads:
        copy.start()
    greet()
    there = held.at[z, y, core]
    copies.send(("sib", 0), ans_ref.at[1 - core], there.at[pieces[0]], sibling())
    copies.send(("sib", 1), pre_ref.at[1 - core], there.at[mine], sibling())
    copies.send(("pair", 0), pre_ref.at[core], there.at[mine], across(True))
    copies.send(("pair", 1), pre_ref.at[1 - core], there.at[mine], across(False))

    def pass_on(key, r, ref, axis, direction):
        target = to(sources[r], direction, 0) if axis == 0 else to(sources[r], 0, direction)
        copies.send(key, ref, ref, target)

    def own(r, piece):
        ref = block(r, 0, 0).at[pieces[piece]]
        for direction in (1, 3):
            pass_on(("one", r, direction, piece), r, ref, 0, direction)
        for direction in (1, 3):
            pass_on(("two", r, 0, direction, piece), r, ref, 1, direction)

    def spread(r, k):
        for direction in (1, 3):
            pass_on(("two", r, k, direction, 2), r, block(r, ORDER[k], 0), 1, direction)

    def keep(r, dp, dq):
        zz, yy = shifted(sources[r], dp, dq)
        store = pltpu.make_async_copy(
            held.at[zz, yy, sources[r]], kv_out.at[zz, yy, sources[r]], out_sem.at[len(stores)]
        )
        store.start()
        stores.append(store)

    loads[0].wait()
    own(0, 0)
    copies.arrived(("sib", 0), block(1, 0, 0).at[pieces[0]], sibling())
    own(1, 0)
    loads[1].wait()
    copies.arrived(("pair", 0), block(0, 0, 0).at[other], across(True))
    own(0, 1)
    keep(0, 0, 0)
    copies.arrived(("sib", 1), block(1, 0, 0).at[mine], sibling())
    copies.arrived(("pair", 1), block(1, 0, 0).at[other], across(False))
    own(1, 1)
    keep(1, 0, 0)
    copies.send(("sib", 2), q_ref.at[1 - core], q_out.at[:, own_rows], sibling())
    copies.send(("sib", 3), g_ref.at[1 - core], g_out.at[:, own_rows], sibling())

    for direction in (1, 3):
        for r in range(2):
            back = (-direction) % RING
            for piece in range(2):
                copies.arrived(
                    ("one", r, direction, piece), block(r, back, 0).at[pieces[piece]], to(sources[r], direction, 0)
                )
            n = direction // 2
            pass_on(("far", r, direction), r, block(r, back, 0).at[parts[n]], 0, direction)
            spread(r, ORDER.index(back))
            keep(r, back, 0)
    for r in range(2):
        for direction in (1, 3):
            copies.arrived(
                ("far", r, direction), block(r, 2, 0).at[parts[direction // 2]], to(sources[r], direction, 0)
            )
        spread(r, 3)
        keep(r, 2, 0)
    for k in range(RING):
        for direction in (1, 3):
            for r in range(2):
                back = (-direction) % RING
                here = block(r, ORDER[k], back)
                for piece in range(2) if k == 0 else (2,):
                    area = here if piece == 2 else here.at[pieces[piece]]
                    copies.arrived(("two", r, k, direction, piece), area, to(sources[r], 0, direction))
                pass_on(("far2", r, k, direction), r, here.at[parts[direction // 2]], 1, direction)
                keep(r, ORDER[k], back)
    for k in range(RING):
        for r in range(2):
            here = block(r, ORDER[k], 2)
            for direction in (1, 3):
                copies.arrived(("far2", r, k, direction), here.at[parts[direction // 2]], to(sources[r], 0, direction))
            keep(r, ORDER[k], 2)
    copies.arrived(("sib", 2), q_out.at[:, sibling_rows], sibling())
    copies.arrived(("sib", 3), g_out.at[:, sibling_rows], sibling())
    loads[2].wait()
    loads[3].wait()
    for store in stores:
        store.wait()
    copies.finish()


def gather(ans, pre, queries, grad_out):
    _, ans_rows, width = ans.shape
    pre_rows = pre.shape[1]
    rows = ans_rows + 2 * pre_rows
    _, batch, pos, features = queries.shape
    anywhere = pl.BlockSpec(memory_space=pl.ANY)
    both = jax.ShapeDtypeStruct((batch, CORES * pos, features), queries.dtype)
    return pl.pallas_call(
        functools.partial(gather_kernel, ans_rows, pre_rows),
        out_shape=(jax.ShapeDtypeStruct((RING, RING, CORES, rows, width), ans.dtype), both, both),
        in_specs=[pl.BlockSpec(memory_space=pltpu.VMEM)] * 4,
        out_specs=(anywhere, anywhere, anywhere),
        scratch_shapes=[
            pltpu.VMEM((RING, RING, CORES, rows, width), ans.dtype),
            pltpu.SemaphoreType.DMA((GATHER_COPIES,)),
            pltpu.SemaphoreType.DMA((GATHER_COPIES,)),
            pltpu.SemaphoreType.DMA((4,)),
            pltpu.SemaphoreType.DMA((2 * RING * RING,)),
        ],
        compiler_params=pltpu.CompilerParams(collective_id=0, has_side_effects=True),
        name="gather",
    )(ans, pre, queries, grad_out)


SCATTER_COPIES = 60


def scatter_kernel(
    ans_rows,
    pre_rows,
    terms_ref,
    att_ref,
    dq_ref,
    ans_out,
    pre_out,
    att_out,
    dq_out,
    total,
    far2,
    near2,
    far1,
    near1,
    ans_swap,
    pre_swap,
    pre_got,
    send_sem,
    recv_sem,
    local_sem,
    out_sem,
):
    z, y, core = place()
    rows, parts, mine, other = spans(ans_rows, pre_rows)
    copies = Copies(send_sem, recv_sem)
    sources = (core, 1 - core)
    order = (2, 1, 3, 0)
    q_order = (2, 1, 3, 0)

    def block(r, dp, dq):
        zz, yy = shifted(sources[r], dp, dq)
        return total.at[zz, yy, sources[r]]

    loads = {}
    for k in range(RING):
        for r in range(2):
            for m in range(RING):
                zz, yy = shifted(sources[r], order[k], q_order[m])
                spot = (zz, yy, sources[r])
                n = len(loads)
                loads[r, k, m] = pltpu.make_async_copy(terms_ref.at[spot], total.at[spot], local_sem.at[n])
                loads[r, k, m].start()
    pos = att_ref.shape[1] // CORES
    own_rows = pl.ds(pl.multiple_of(core * pos, pos), pos)
    sibling_rows = pl.ds(pl.multiple_of((1 - core) * pos, pos), pos)
    greet()
    for k in range(RING):
        for r in range(2):
            loads[r, k, 0].wait()
            for n, direction in enumerate((1, 3)):
                copies.send(
                    ("far2", r, k, n),
                    block(r, order[k], 2).at[parts[n]],
                    far2.at[r, k, n],
                    to(sources[r], 0, direction),
                )
    outs = [
        pltpu.make_async_copy(att_ref.at[:, own_rows], att_out.at[core], out_sem.at[0]),
        pltpu.make_async_copy(dq_ref.at[:, own_rows], dq_out.at[core], out_sem.at[1]),
    ]
    for copy in outs:
        copy.start()
    copies.send(("sib", 0), att_ref.at[:, sibling_rows], att_out.at[core], sibling())
    copies.send(("sib", 1), dq_ref.at[:, sibling_rows], dq_out.at[core], sibling())

    def add(into, other_ref):
        into[...] = (into[...].astype(F32) + other_ref[...].astype(F32)).astype(BF16)

    for k in range(RING):
        for r in range(2):
            for n, direction in enumerate((1, 3)):
                loads[r, k, 1 + n].wait()
                here = block(r, order[k], direction)
                copies.arrived(("far2", r, k, n), far2.at[r, k, n], to(sources[r], 0, direction))
                add(here.at[parts[n]], far2.at[r, k, n])
                copies.send(("near2", r, k, n), here, near2.at[r, k, n], to(sources[r], 0, direction))

    def settle2(r, k):
        loads[r, k, 3].wait()
        for n, direction in enumerate((1, 3)):
            copies.arrived(("near2", r, k, n), near2.at[r, k, n], to(sources[r], 0, direction))
        into = block(r, order[k], 0)
        into[...] = (
            into[...].astype(F32) + near2[r, k, 0].astype(F32) + near2[r, k, 1].astype(F32)
        ).astype(BF16)

    for r in range(2):
        settle2(r, 0)
        for n, direction in enumerate((1, 3)):
            copies.send(("far1", r, n), block(r, 2, 0).at[parts[n]], far1.at[r, n], to(sources[r], direction, 0))
    for k in (1, 2):
        n = k - 1
        direction = order[k]
        for r in range(2):
            settle2(r, k)
            here = block(r, direction, 0)
            copies.arrived(("far1", r, n), far1.at[r, n], to(sources[r], direction, 0))
            add(here.at[parts[n]], far1.at[r, n])
            copies.send(("near1", r, n), here, near1.at[r, n], to(sources[r], direction, 0))
    for r in range(2):
        settle2(r, 3)
    for r in (1, 0):
        for n, direction in enumerate((1, 3)):
            copies.arrived(("near1", r, n), near1.at[r, n], to(sources[r], direction, 0))
        here = block(r, 0, 0)

        def final(area):
            return (
                here[area].astype(F32) + near1[r, 0, area].astype(F32) + near1[r, 1, area].astype(F32)
            )

        pre_swap[r, 0] = final(other).astype(BF16)
        if r == 1:
            copies.send(("pre", 1, 0), pre_swap.at[1, 0], pre_got.at[1, 0], across(False))
            pre_swap[1, 1] = final(mine).astype(BF16)
            copies.send(("pre", 1, 1), pre_swap.at[1, 1], pre_got.at[1, 1], sibling())
            ans_swap[...] = final(pl.ds(0, ans_rows)).astype(BF16)
            copies.send(("ans",), ans_swap, ans_out.at[core], sibling())
        else:
            copies.send(("pre", 0, 0), pre_swap.at[0, 0], pre_got.at[0, 0], across(True))
            pre_out[core] = final(mine)
            ans_out[core] = final(pl.ds(0, ans_rows)).astype(BF16)
    copies.arrived(("pre", 1, 1), pre_got.at[1, 1], sibling())
    copies.arrived(("pre", 1, 0), pre_got.at[1, 0], across(False))
    pre_out[1 - core] = pre_got[1, 0].astype(F32) + pre_got[1, 1].astype(F32)
    copies.arrived(("pre", 0, 0), pre_got.at[0, 0], across(True))
    pre_out[core] = pre_out[core] + pre_got[0, 0].astype(F32)
    copies.arrived(("ans",), ans_out.at[1 - core], sibling())
    copies.arrived(("sib", 0), att_out.at[1 - core], sibling())
    copies.arrived(("sib", 1), dq_out.at[1 - core], sibling())
    for copy in outs:
        copy.wait()
    copies.finish()


def scatter(terms, attended, grad_queries, ans_rows, pre_rows):
    rows, width = terms.shape[-2:]
    half = rows // 2
    batch, pos2, features = attended.shape
    split = jax.ShapeDtypeStruct((CORES, batch, pos2 // CORES, features), attended.dtype)
    vmem = pl.BlockSpec(memory_space=pltpu.VMEM)
    anywhere = pl.BlockSpec(memory_space=pl.ANY)
    return pl.pallas_call(
        functools.partial(scatter_kernel, ans_rows, pre_rows),
        out_shape=(
            jax.ShapeDtypeStruct((CORES, ans_rows, width), BF16),
            jax.ShapeDtypeStruct((CORES, pre_rows, width), F32),
            split,
            split,
        ),
        in_specs=[anywhere, vmem, vmem],
        out_specs=(vmem, vmem, anywhere, anywhere),
        scratch_shapes=[
            pltpu.VMEM((RING, RING, CORES, rows, width), BF16),
            pltpu.VMEM((CORES, RING, 2, half, width), BF16),
            pltpu.VMEM((CORES, RING, 2, rows, width), BF16),
            pltpu.VMEM((CORES, 2, half, width), BF16),
            pltpu.VMEM((CORES, 2, rows, width), BF16),
            pltpu.VMEM((ans_rows, width), BF16),
            pltpu.VMEM((2, 2, pre_rows, width), BF16),
            pltpu.VMEM((2, 2, pre_rows, width), BF16),
            pltpu.SemaphoreType.DMA((SCATTER_COPIES,)),
            pltpu.SemaphoreType.DMA((SCATTER_COPIES,)),
            pltpu.SemaphoreType.DMA((2 * RING * RING,)),
            pltpu.SemaphoreType.DMA((2,)),
        ],
        compiler_params=pltpu.CompilerParams(collective_id=1, has_side_effects=True),
        name="scatter",
    )(terms, attended, grad_queries)


def nn(a, b):
    return lax.dot_general(a, b, (((1,), (0,)), ((), ())), preferred_element_type=F32)


def nt(a, b):
    return lax.dot_general(a, b, (((1,), (1,)), ((), ())), preferred_element_type=F32)


ANS_SOURCES = 4
PRE_SOURCES = 8


def attend_kernel(
    ans_here,
    pre_rows,
    group,
    length_ref,
    limit_ref,
    q_ref,
    g_ref,
    kv_ref,
    out_ref,
    dq_ref,
    terms_ref,
    scores,
    weights,
    queries,
    douts,
    queries_t,
    douts_t,
    prefix_terms,
    top,
    row_sum,
    acc_t,
):
    sources = kv_ref.shape[0]
    d = HEAD_DIM
    b = pl.program_id(0)
    s = lax.axis_index("seq")
    scale = d**-0.5
    here_rows = CORES * ans_here
    rows = group * here_rows
    ans_chunk = ANS_SOURCES * ans_here
    pre_chunk = PRE_SOURCES * pre_rows
    per_pair = sources // PRE_SOURCES
    pre_total = 2 * sources * pre_rows
    first_row = (s // CORES) * here_rows
    length = length_ref[0, b]
    limit = limit_ref[0, b]
    ans_at = pl.multiple_of(b * ans_here, ans_here)
    live_here = first_row < length
    n_pre = jnp.where(live_here, (limit + pre_chunk - 1) // pre_chunk, 0)
    n_full = jnp.where(live_here, limit // pre_chunk, 0)
    n_ans = jnp.where(live_here, (s // CORES) * CORES // ANS_SOURCES + 1, 0)

    @pl.when(b == 0)
    def _():
        prefix_terms[...] = jnp.zeros_like(prefix_terms)

    terms_ref[:, pl.ds(ans_at, ans_here), :] = jnp.zeros((sources, ans_here, 2 * d), BF16)

    def pre_block(i, lanes):
        pair_at, source = i // per_pair, (i % per_pair) * PRE_SOURCES
        row = pl.multiple_of(2 * ans_here + pair_at * pre_rows, 16)
        part = kv_ref[pl.ds(source, PRE_SOURCES), pl.ds(row, pre_rows), lanes]
        return part.reshape(pre_chunk, d)

    def ans_block(i, lanes):
        part = kv_ref[pl.ds(i * ANS_SOURCES, ANS_SOURCES), pl.ds(ans_at, ans_here), lanes]
        return part.reshape(ans_chunk, d)

    keys_at, values_at = slice(0, d), slice(d, 2 * d)

    def pre_span(i):
        return pl.ds(pl.multiple_of(i * pre_chunk, pre_chunk), pre_chunk)

    def ans_span(i):
        return pl.ds(pl.multiple_of(pre_total + i * ans_chunk, ans_chunk), ans_chunk)

    def fold(values, into):
        return jnp.maximum(into, jnp.max(values.reshape(values.shape[0] // 8, 8, rows), axis=0))

    @pl.when(live_here)
    def _():
        place_rows = lax.broadcasted_iota(jnp.int32, (here_rows, d), 0)
        alive = place_rows + first_row < length
        for g in range(group):
            lanes = slice(g * d, (g + 1) * d)
            here = slice(g * here_rows, (g + 1) * here_rows)
            queries[here] = q_ref[0, :, lanes]
            douts[here] = jnp.where(alive, g_ref[0, :, lanes].astype(F32), 0.0)
        douts_t[...] = douts[...].T
        top[...] = jnp.full_like(top, NEGATIVE)

        def score(i, block, span, keep):
            values = nt(block(i, keys_at), queries[...])
            if keep is not None:
                values = jnp.where(keep(i, values.shape), values, NEGATIVE)
            scores[span(i)] = values
            top[...] = fold(values, top[...])

        def pre_keep(i, shape):
            return lax.broadcasted_iota(jnp.int32, shape, 0) + i * pre_chunk < limit

        def ans_keep(i, shape):
            key = lax.broadcasted_iota(jnp.int32, shape, 0) + i * ans_chunk
            row = lax.broadcasted_iota(jnp.int32, shape, 1) % here_rows + first_row
            return key <= row

        @pl.loop(0, n_full)
        def _(i):
            score(i, pre_block, pre_span, None)

        @pl.when(n_full < n_pre)
        def _():
            score(n_full, pre_block, pre_span, pre_keep)

        @pl.loop(0, n_ans - 1)
        def _(i):
            score(i, ans_block, ans_span, None)

        score(n_ans - 1, ans_block, ans_span, ans_keep)

        top_row = jnp.max(top[...], axis=0, keepdims=True)
        shift = top_row * (scale * LOG2E)
        row_sum[...] = jnp.zeros_like(row_sum)
        acc_t[...] = jnp.zeros_like(acc_t)

        def spread(i, block, span):
            e = jnp.exp2(scores[span(i)] * (scale * LOG2E) - shift)
            row_sum[...] += jnp.sum(e.reshape(e.shape[0] // 8, 8, rows), axis=0)
            low = e.astype(BF16)
            weights[span(i)] = low
            acc_t[...] += nn(block(i, values_at).T, low)

        @pl.loop(0, n_pre)
        def _(i):
            spread(i, pre_block, pre_span)

        @pl.loop(0, n_ans)
        def _(i):
            spread(i, ans_block, ans_span)

        inverse = 1.0 / jnp.sum(row_sum[...], axis=0, keepdims=True)
        attended_t = acc_t[...] * inverse
        scaled = (douts_t[...] * inverse).astype(BF16)
        delta = jnp.sum(scaled.astype(F32) * attended_t, axis=0, keepdims=True)
        douts_low_t = scaled
        queries_t[...] = douts_low_t
        douts_low = douts_low_t.astype(F32).T.astype(BF16)
        attended = attended_t.T
        for g in range(group):
            lanes = slice(g * d, (g + 1) * d)
            here = slice(g * here_rows, (g + 1) * here_rows)
            out_ref[0, :, lanes] = jnp.where(alive, attended[here], 0.0).astype(BF16)
        douts[...] = douts_low.astype(F32)
        acc_t[...] = jnp.zeros_like(acc_t)

        def back(i, block, span):
            low = weights[span(i)]
            grad_probs = nn(block(i, values_at), queries_t[...])
            grad_low = (low.astype(F32) * (grad_probs - delta)).astype(BF16)
            value_term = nn(low, douts_low)
            key_term = nn(grad_low, queries[...]) * scale
            acc_t[...] += nn(block(i, keys_at).T, grad_low)
            return key_term, value_term

        @pl.loop(0, n_pre)
        def _(i):
            key_term, value_term = back(i, pre_block, pre_span)
            prefix_terms[pre_span(i), 0:d] += key_term
            prefix_terms[pre_span(i), d : 2 * d] += value_term

        @pl.loop(0, n_ans)
        def _(i):
            key_term, value_term = back(i, ans_block, ans_span)
            at = pl.ds(i * ANS_SOURCES, ANS_SOURCES)
            span = pl.ds(ans_at, ans_here)
            terms_ref[at, span, 0:d] = key_term.astype(BF16).reshape(ANS_SOURCES, ans_here, d)
            terms_ref[at, span, d : 2 * d] = value_term.astype(BF16).reshape(ANS_SOURCES, ans_here, d)

        grad_queries = (acc_t[...] * scale).T
        for g in range(group):
            lanes = slice(g * d, (g + 1) * d)
            here = slice(g * here_rows, (g + 1) * here_rows)
            dq_ref[0, :, lanes] = grad_queries[here].astype(BF16)

    @pl.when(jnp.logical_not(live_here))
    def _():
        out_ref[...] = jnp.zeros_like(out_ref)
        dq_ref[...] = jnp.zeros_like(dq_ref)

    @pl.when(b == 1)
    def _():
        @pl.loop(0, 2 * per_pair)
        def _(i):
            pair_at, source = i // per_pair, (i % per_pair) * PRE_SOURCES
            row = pl.multiple_of(2 * ans_here + pair_at * pre_rows, 16)
            terms_ref[pl.ds(source, PRE_SOURCES), pl.ds(row, pre_rows), :] = (
                prefix_terms[pre_span(i)].astype(BF16).reshape(PRE_SOURCES, pre_rows, 2 * d)
            )


def attend(queries, grad_out, gathered, lengths, limits, ans_here, pre_rows):
    batch, here_rows, features = queries.shape
    sources, rows_all, width = gathered.shape
    d = HEAD_DIM
    group = features // d
    keys_total = sources * ans_here + 2 * sources * pre_rows
    rows = group * here_rows
    query_spec = pl.BlockSpec((1, here_rows, features), lambda b: (b, 0, 0))
    kv_spec = pl.BlockSpec((sources, rows_all, width), lambda b: (0, 0, 0))
    smem = pl.BlockSpec(memory_space=pltpu.SMEM)
    return pl.pallas_call(
        functools.partial(attend_kernel, ans_here, pre_rows, group),
        grid=(batch,),
        out_shape=(
            jax.ShapeDtypeStruct(queries.shape, BF16),
            jax.ShapeDtypeStruct(queries.shape, BF16),
            jax.ShapeDtypeStruct(gathered.shape, BF16),
        ),
        in_specs=[smem, smem, query_spec, query_spec, kv_spec],
        out_specs=(query_spec, query_spec, kv_spec),
        scratch_shapes=[
            pltpu.VMEM((keys_total, rows), F32),
            pltpu.VMEM((keys_total, rows), BF16),
            pltpu.VMEM((rows, d), BF16),
            pltpu.VMEM((rows, d), F32),
            pltpu.VMEM((d, rows), BF16),
            pltpu.VMEM((d, rows), F32),
            pltpu.VMEM((2 * sources * pre_rows, width), F32),
            pltpu.VMEM((8, rows), F32),
            pltpu.VMEM((8, rows), F32),
            pltpu.VMEM((d, rows), F32),
        ],
        compiler_params=pltpu.CompilerParams(
            dimension_semantics=("arbitrary",), vmem_limit_bytes=60 * 1024 * 1024
        ),
        name="attend",
    )(lengths, limits, queries, grad_out, gathered)


def on_device(
    queries,
    answer_keys,
    answer_values,
    prefix_keys,
    prefix_values,
    grad_out,
    answer_length,
    prefix_limit,
):
    d = HEAD_DIM
    _, ans_here, batch, features = queries.shape
    kv = answer_keys.shape[3] // d
    pre_rows = prefix_keys.shape[0]
    side = lax.axis_size("seq")

    def by_head(keys, values):
        both = jnp.stack([keys.reshape(-1, kv, d), values.reshape(-1, kv, d)], axis=2)
        return both.transpose(1, 0, 2, 3).reshape(kv, -1, 2 * d)

    def batch_first(x):
        return x[0].transpose(1, 0, 2)

    def head_first(x):
        return x[0].reshape(ans_here, batch, kv, features // kv).transpose(2, 1, 0, 3)

    ans = by_head(batch_first(answer_keys), batch_first(answer_values))
    pre = by_head(prefix_keys, prefix_values)
    gathered, q_here, g_here = gather(ans, pre, head_first(queries), head_first(grad_out))
    flat = gathered.reshape(side, gathered.shape[-2], 2 * d)
    attended, grad_q, terms = attend(q_here, g_here, flat, answer_length, prefix_limit, ans_here, pre_rows)
    ans_sums, pre_sums, out, grad_queries = scatter(
        terms.reshape(gathered.shape), attended, grad_q, batch * ans_here, pre_rows
    )

    def back(x):
        return x.transpose(2, 1, 0, 3).reshape(queries.shape)

    def apart(x, n):
        return x[:, :, n * d : (n + 1) * d]

    def ans_grad(n):
        x = apart(ans_sums, n).reshape(kv, batch, ans_here, d).transpose(2, 1, 0, 3)
        return x.reshape(answer_keys.shape)

    def pre_grad(n):
        return apart(pre_sums, n).transpose(1, 0, 2).reshape(prefix_keys.shape)

    return (back(out), back(grad_queries), ans_grad(0), ans_grad(1), pre_grad(0), pre_grad(1))


def solution(mesh):
    tokens = P("pair", "seq", None, "head")
    prefix = P(("pair", "seq"), "head")
    scalars = P("pair", None)
    return jax.shard_map(
        on_device,
        mesh=mesh,
        in_specs=(tokens, tokens, tokens, prefix, prefix, tokens, scalars, scalars),
        out_specs=(tokens, tokens, tokens, tokens, prefix, prefix),
        check_vma=False,
    )
```

time: 134 us -> 121 us (0.903)
  the two profiles are of different devices: /device:TPU:1 before, /device:TPU:32 now
where the time goes in v2:
time: 121 us; the launch traced here: 119 us
  Pallas kernels  101 us (83%)
  local copies, waits for them, and re-layouts  16.5 us (14%)
    pallas_call x1, Pallas kernels, scatter(): pl.pallas_call(functools.partial(scatter_kernel, ans_rows, pre_rows), out...  40.5 us
    pallas_call x1, Pallas kernels, gather(): pl.pallas_call(functools.partial(gather_kernel, ans_rows, pre_rows), out_...  32.2 us
    pallas_call x1, Pallas kernels, attend(): pl.pallas_call(functools.partial(attend_kernel, ans_here, pre_rows, group...  28.6 us
    unnamed x9, local copies, waits for them, and re-layouts  5.15 us
    another operation x2, local copies, waits for them, and re-layouts, head_first(): x[0].reshape(ans_here, batch, kv, features // kv).transpose(2, 1, 0, 3)  2.62 us

profile of v2, /device:TPU:32, one launch (start us, length us, event | category | flops | bytes accessed | tf_op | source)
XLA Modules:
  0.0 118.8 jit_solution(2860294508785243846)
XLA Ops:
  0.6 0.8 stack_reshape.14
  1.4 0.8 stack_reshape.15
  2.2 0.1 maximum_bitcast_fusion.1
  2.4 0.7 reshape.49.pre_ref
  3.0 0.8 copy.18
  3.9 0.9 copy.19
  4.8 0.2 maximum_bitcast_fusion
  5.0 0.1 copy.20
  5.1 0.7 reshape.48.ans_ref
  5.8 1.3 %reshape.60 = bf16[64,2,2,896]{3,2,1,0:T(2,128)(2,1)S(1)} reshape(bf16[1,64,2,1792]{3,2,1,0:T(2,128)(2,1)} %param.8) | data formatting | bytes 917504 | tf_op jit(solution)/shard_map/reshape;squeeze | solution.py:683
  7.2 1.3 %reshape.61 = bf16[64,2,2,896]{3,2,1,0:T(2,128)(2,1)S(1)} reshape(bf16[1,64,2,1792]{3,2,1,0:T(2,128)(2,1)} %param.13) | data formatting | bytes 917504 | tf_op jit(solution)/shard_map/reshape;squeeze | solution.py:683
  8.5 1.1 copy_bitcast_fusion
  9.5 32.2 %gather.1 = (bf16[4,4,2,224,256]{4,3,2,1,0:T(8,128)(2,1)}, bf16[2,128,896]{2,1,0:T(8,128)(2,1)}, bf16[2,128,896]{2,1,0:T(8,128)(2,1)}) custom-call(bf16[2,128,256]{2,1,0:T(8,128)(2,1)} %reshape.48.ans_ref, bf16[2,48,256]{2,1,0:T(8,128)(2,1)} %reshape.49.pre_ref, bf16[2,2,64,896]{3,2,1,0:T(8,128)(2,1)} %get-tuple-element.37.q_ref, ...), custom_call_target="tpu_custom_call" | custom-call | tf_op jit(solution)/shard_map/gather/pallas_call | solution.py:225
  41.7 28.6 %attend.1 = (bf16[2,128,896]{2,1,0:T(8,128)(2,1)}, bf16[2,128,896]{2,1,0:T(8,128)(2,1)}, bf16[32,224,256]{2,1,0:T(8,128)(2,1)}) custom-call(s32[1,2]{1,0:T(1,128)} %length_ref.1, s32[1,2]{1,0:T(1,128)} %limit_ref.1, bf16[2,128,896]{2,1,0:T(8,128)(2,1)} %get-tuple-element.16.q_ref, bf16[2,128,896]{2,1,0:T(8,128)(2,1)} %get-tuple-element.17.g_ref, ...), custom_call_target="tpu_custom_call" | custom-call | tf_op jit(solution)/shard_map/attend/pallas_call | solution.py:630
  70.3 40.5 %scatter.1 = (bf16[2,128,256]{2,1,0:T(8,128)(2,1)}, f32[2,48,256]{2,1,0:T(8,128)}, bf16[2,2,64,896]{3,2,1,0:T(8,128)(2,1)}, bf16[2,2,64,896]{3,2,1,0:T(8,128)(2,1)}) custom-call(bf16[4,4,2,224,256]{4,3,2,1,0:T(8,128)(2,1)} %bitcast.37, bf16[2,128,896]{2,1,0:T(8,128)(2,1)} %get-tuple-element.20.att_ref, bf16[2,128,896]{2,1,0:T(8,128)(2,1)} %get-tuple-element.21.dq_ref), custom_call_target="tpu_custom_call" | custom-call | tf_op jit(solution)/shard_map/scatter/pallas_call | solution.py:388
  110.8 0.0 copy-start.1
  110.8 0.0 copy-start
  110.9 1.5 %copy.39 = bf16[64,2,2,896]{3,2,1,0:T(2,128)(2,1)S(1)} copy(bf16[64,2,2,896]{3,0,1,2:T(8,128)(2,1)} %bitcast.39) | data formatting | bytes 917504
  112.4 1.1 reshape.62
  113.4 1.5 %copy.40 = bf16[64,2,2,896]{3,2,1,0:T(2,128)(2,1)S(1)} copy(bf16[64,2,2,896]{3,0,1,2:T(8,128)(2,1)} %bitcast.38) | data formatting | bytes 917504
  114.9 1.1 reshape.63
  116.0 0.0 copy-done.1
  116.0 0.6 copy.49
  116.6 0.6 copy.50
  117.3 0.0 copy-done
  117.3 0.1 copy.30
  117.4 0.7 reshape.57
  118.0 0.1 copy.29
  118.1 0.7 reshape.55
  (6 shorter events, 0.2 us)
Async XLA Ops:
  110.8 5.2 %copy-start.1 = (f32[2,48,256]{2,1,0:T(8,128)S(1)}, f32[2,48,256]{2,1,0:T(8,128)}, u32[]{:S(2)}) copy-start(f32[2,48,256]{2,1,0:T(8,128)} %get-tuple-element.25) | copy-start | bytes 294916
  110.8 6.4 %copy-start = (bf16[2,128,256]{2,1,0:T(8,128)(2,1)S(1)}, bf16[2,128,256]{2,1,0:T(8,128)(2,1)}, u32[]{:S(2)}) copy-start(bf16[2,128,256]{2,1,0:T(8,128)(2,1)} %get-tuple-element.24) | copy-start | bytes 393220

commit v3 on v0

v3 whole, which is shorter than its diff:
```python
import functools

import jax
import jax.numpy as jnp
from jax import lax
from jax.experimental import pallas as pl
from jax.experimental.pallas import tpu as pltpu
from jax.sharding import PartitionSpec as P

HEAD_DIM = 128
RING = 4
CORES = 2
LOG2E = 1.4426950408889634
NEGATIVE = -1e30
MESH = pl.DeviceIdType.MESH
BF16 = jnp.bfloat16
F32 = jnp.float32


def place():
    s = lax.axis_index("seq")
    return s // (RING * CORES), (s // CORES) % RING, s % CORES


def seq_of(z, y, core):
    return (z * RING + y) * CORES + core


def shifted(h, dp, dq):
    z, y, _ = place()
    return (z + dp * h + dq * (1 - h)) % RING, (y + dp * (1 - h) + dq * h) % RING


def to(h, dp, dq):
    z, y = shifted(h, dp, dq)
    return {"seq": seq_of(z, y, place()[2])}


def across(same_core):
    z, y, core = place()
    target = {"pair": 1 - lax.axis_index("pair")}
    if not same_core:
        target["seq"] = seq_of(z, y, 1 - core)
    return target


def sibling():
    z, y, core = place()
    return {"seq": seq_of(z, y, 1 - core)}


PEERS = 7


def greet():
    barrier = pltpu.get_barrier_semaphore()
    peers = [to(h, d, 0) for h in range(2) for d in (1, RING - 1)]
    peers += [sibling(), across(True), across(False)]
    for peer in peers:
        pl.semaphore_signal(barrier, inc=1, device_id=peer, device_id_type=MESH)


def met():
    pl.semaphore_wait(pltpu.get_barrier_semaphore(), PEERS)


def spans(ans_rows, pre_rows):
    pair = lax.axis_index("pair")
    rows = ans_rows + 2 * pre_rows
    half = rows // 2
    parts = (pl.ds(0, half), pl.ds(half, rows - half))
    mine = pl.ds(pl.multiple_of(ans_rows + pair * pre_rows, 16), pre_rows)
    other = pl.ds(pl.multiple_of(ans_rows + (1 - pair) * pre_rows, 16), pre_rows)
    return rows, parts, mine, other


class Copies:
    def __init__(self, send_sem, recv_sem):
        self.send_sem, self.recv_sem = send_sem, recv_sem
        self.ids = {}
        self.sent = []

    def make(self, key, src, dst, to):
        n = self.ids.setdefault(key, len(self.ids))
        return pltpu.make_async_remote_copy(
            src_ref=src,
            dst_ref=dst,
            send_sem=self.send_sem.at[n],
            recv_sem=self.recv_sem.at[n],
            device_id=to,
            device_id_type=MESH,
        )

    def send(self, key, ends):
        self.make(key, *ends()).start()
        self.sent.append((key, ends))

    def arrived(self, key, dst, to):
        self.make(key, dst, dst, to).wait_recv()

    def finish(self):
        for key, ends in self.sent:
            self.make(key, *ends()).wait_send()


def pick(i, values):
    chosen = jnp.int32(values[0])
    for n in range(1, len(values)):
        chosen = jnp.where(i == n, jnp.int32(values[n]), chosen)
    return chosen


def run_at(condition, step):
    @pl.when(condition)
    def _():
        step()


def nn(a, b):
    return lax.dot_general(a, b, (((1,), (0,)), ((), ())), preferred_element_type=F32)


def nt(a, b):
    return lax.dot_general(a, b, (((1,), (1,)), ((), ())), preferred_element_type=F32)


COPIES = 104
ORDER = (0, 3, 1, 2)
FORWARD = (
    (0, 0), (3, 0), (1, 0), (0, 3), (0, 1), (2, 0), (3, 3), (3, 1),
    (1, 3), (1, 1), (0, 2), (2, 3), (2, 1), (3, 2), (1, 2), (2, 2),
)
BACK_P = (2, 1, 3, 0)
BACKWARD = (
    (0, 2), (1, 2), (0, 1), (0, 3), (2, 2), (1, 1), (1, 3), (0, 0),
    (3, 2), (2, 1), (2, 3), (1, 0), (3, 1), (3, 3), (2, 0), (3, 0),
)


def layer_kernel(
    group,
    length_ref,
    limit_ref,
    ak_ref,
    av_ref,
    pk_ref,
    pv_ref,
    q_ref,
    g_ref,
    att_final,
    dq_final,
    ak_final,
    av_final,
    pk_final,
    pv_final,
    held,
    total,
    staged_ans,
    staged_pre,
    answers_in,
    prefix_in,
    native,
    split,
    rows_ref,
    weights,
    tops,
    top_now,
    row_sum,
    acc_t,
    douts,
    douts_t,
    delta_ref,
    masked_queries,
    probs_low,
    fin,
    ans_out,
    pre_out,
    far2,
    near2,
    far1,
    near1,
    ans_swap,
    pre_swap,
    pre_got,
    send_sem,
    recv_sem,
    local_sem,
):
    d = HEAD_DIM
    z, y, core = place()
    pos = q_ref.shape[1]
    batch = q_ref.shape[2]
    ans_rows = batch * pos
    pre_rows = pk_ref.shape[0]
    sources_total = RING * RING * CORES
    here_rows = CORES * pos
    rows = group * here_rows
    scale = d**-0.5
    factor = scale * LOG2E
    chip = z * RING + y
    pair = lax.axis_index("pair")
    block_rows, parts, mine, other = spans(ans_rows, pre_rows)
    pieces = (pl.ds(0, ans_rows), pl.ds(ans_rows, 2 * pre_rows))
    copies = Copies(send_sem, recv_sem)
    sources = (core, 1 - core)

    def held_at(r, dp, dq):
        zz, yy = shifted(sources[r], dp, dq)
        return held.at[zz, yy, sources[r]]

    def total_at(r, dp, dq):
        zz, yy = shifted(sources[r], dp, dq)
        return total.at[zz, yy, sources[r]]

    greet()
    small_fetches = [
        pltpu.make_async_copy(ref, small, local_sem.at[6 + n])
        for n, (ref, small) in enumerate(
            zip((ak_ref, av_ref, pk_ref, pv_ref), (answers_in.at[0], answers_in.at[1], prefix_in.at[0], prefix_in.at[1]))
        )
    ]

    def fetch(n):
        return pltpu.make_async_copy((q_ref, g_ref)[n].at[0], native.at[n], local_sem.at[n])

    for copy in small_fetches + [fetch(0), fetch(1)]:
        copy.start()
    for copy in small_fetches:
        copy.wait()
    for n in range(2):
        lanes = slice(n * d, (n + 1) * d)
        for c in range(CORES):
            head = slice(c * d, (c + 1) * d)
            staged_ans[c, :, lanes] = jnp.swapaxes(answers_in[n, 0, :, :, head], 0, 1).reshape(ans_rows, d)
            staged_pre[c, :, lanes] = prefix_in[n, :, head]
    met()
    loads = [
        pltpu.make_async_copy(staged_ans.at[core], held.at[z, y, core, pieces[0]], local_sem.at[2]),
        pltpu.make_async_copy(staged_pre.at[core], held.at[z, y, core, mine], local_sem.at[3]),
    ]
    for copy in loads:
        copy.start()
    there = held.at[z, y, core]
    copies.send(("sib", 0), lambda: (staged_ans.at[1 - core], there.at[pieces[0]], sibling()))
    copies.send(("sib", 1), lambda: (staged_pre.at[1 - core], there.at[mine], sibling()))
    copies.send(("pair", 0), lambda: (staged_pre.at[core], there.at[mine], across(True)))
    copies.send(("pair", 1), lambda: (staged_pre.at[1 - core], there.at[mine], across(False)))

    def own(r, piece):
        ref = held_at(r, 0, 0).at[pieces[piece]]
        source = staged_ans.at[core] if (r, piece) == (0, 0) else ref
        for direction in (1, 3):
            copies.send(
                ("one", r, direction, piece), lambda direction=direction: (source, ref, to(sources[r], direction, 0))
            )
        for direction in (1, 3):
            copies.send(
                ("two", r, 0, direction, piece), lambda direction=direction: (source, ref, to(sources[r], 0, direction))
            )

    def spread(k):
        for r in range(2):
            for direction in (1, 3):

                def ends(r=r, direction=direction):
                    ref = held_at(r, ORDER[k], 0)
                    return ref, ref, to(sources[r], 0, direction)

                copies.send(("two", r, k, direction, 2), ends)

    def head_lanes(c, g):
        return pl.ds(pl.multiple_of((c * group + g) * d, d), d)

    def lay_out(n):
        fetch(n).wait()
        for g in range(group):
            split[n, :, g] = jnp.swapaxes(native[n, :, :, head_lanes(1 - core, g)], 0, 1)
        copies.send(("q", n), lambda: (split.at[n], rows_ref.at[n, :, :, core], sibling()))
        for g in range(group):
            rows_ref[n, :, g, core] = jnp.swapaxes(native[n, :, :, head_lanes(core, g)], 0, 1)

    def laid_out(n):
        copies.arrived(("q", n), rows_ref.at[n, :, :, 1 - core], sibling())

    own(0, 0)
    lay_out(0)
    copies.arrived(("sib", 0), held_at(1, 0, 0).at[pieces[0]], sibling())
    own(1, 0)
    for copy in loads:
        copy.wait()
    copies.arrived(("pair", 0), held_at(0, 0, 0).at[other], across(True))
    own(0, 1)
    copies.arrived(("sib", 1), held_at(1, 0, 0).at[mine], sibling())
    copies.arrived(("pair", 1), held_at(1, 0, 0).at[other], across(False))
    own(1, 1)
    laid_out(0)

    def first_neighbours():
        for direction in (1, 3):
            back = (-direction) % RING
            for r in range(2):
                for piece in range(2):
                    copies.arrived(
                        ("one", r, direction, piece),
                        held_at(r, back, 0).at[pieces[piece]],
                        to(sources[r], direction, 0),
                    )

                def ends(r=r, direction=direction, back=back):
                    ref = held_at(r, back, 0).at[parts[direction // 2]]
                    return ref, ref, to(sources[r], direction, 0)

                copies.send(("far", r, direction), ends)
            spread(ORDER.index(back))

    def first_far():
        for r in range(2):
            for direction in (1, 3):
                copies.arrived(
                    ("far", r, direction), held_at(r, 2, 0).at[parts[direction // 2]], to(sources[r], direction, 0)
                )
        spread(3)

    def second_neighbours(k):
        for direction in (1, 3):
            back = (-direction) % RING
            for r in range(2):
                here = held_at(r, ORDER[k], back)
                for piece in range(2) if k == 0 else (2,):
                    area = here if piece == 2 else here.at[pieces[piece]]
                    copies.arrived(("two", r, k, direction, piece), area, to(sources[r], 0, direction))

                def ends(r=r, direction=direction, back=back):
                    ref = held_at(r, ORDER[k], back).at[parts[direction // 2]]
                    return ref, ref, to(sources[r], 0, direction)

                copies.send(("far2", r, k, direction), ends)

    def second_far(k):
        for r in range(2):
            here = held_at(r, ORDER[k], 2)
            for direction in (1, 3):
                copies.arrived(("far2", r, k, direction), here.at[parts[direction // 2]], to(sources[r], 0, direction))

    forward_steps = {
        1: first_neighbours,
        2: lambda: lay_out(1),
        3: lambda: second_neighbours(0),
        5: first_far,
        6: lambda: second_neighbours(1),
        8: lambda: second_neighbours(2),
        10: lambda: second_far(0),
        11: lambda: second_neighbours(3),
        13: lambda: second_far(1),
        14: lambda: second_far(2),
        15: lambda: second_far(3),
    }
    top_now[...] = jnp.full_like(top_now, NEGATIVE)
    row_sum[...] = jnp.zeros_like(row_sum)
    acc_t[...] = jnp.zeros_like(acc_t)

    def cat(b, dp, dq, lanes):
        spots = [held_at(r, dp, dq) for r in range(2)]
        return jnp.concatenate(
            [spot[b * pos : (b + 1) * pos, lanes] for spot in spots] + [spot[ans_rows:block_rows, lanes] for spot in spots],
            axis=0,
        )

    keys_at, values_at = slice(0, d), slice(d, 2 * d)

    def mask_features(b, dp, dq):
        limit = limit_ref[0, b]

        def one_hot(feature):
            lane = lax.broadcasted_iota(jnp.int32, feature.shape, 1)
            return jnp.where(lane == feature, 1.0, 0.0)

        ans_part, pre_part = [], []
        for r in range(2):
            zz, yy = shifted(sources[r], dp, dq)
            source = (zz * RING + yy) * CORES + sources[r]
            key = lax.broadcasted_iota(jnp.int32, (pos, d), 0) + (source * pos - chip * here_rows)
            ans_part.append(one_hot(jnp.where(key <= 0, -1, jnp.where(key < here_rows, key, 0))))
            for p in range(2):
                token = lax.broadcasted_iota(jnp.int32, (pre_rows, d), 0) + (p * sources_total + source) * pre_rows
                pre_part.append(one_hot(jnp.where(token < limit, -1, 0)))
        return jnp.concatenate(ans_part + pre_part, axis=0).astype(BF16)

    def query_rows(n, b):
        return rows_ref[n, b].reshape(rows, d)

    tiles = [slice(lo, min(lo + 2 * d, rows)) for lo in range(0, rows, 2 * d)]
    mask_row = lax.broadcasted_iota(jnp.int32, (here_rows, d), 0)
    mask_lane = lax.broadcasted_iota(jnp.int32, (here_rows, d), 1)
    row_mask = jnp.where((mask_lane == 0) | (mask_lane > mask_row), NEGATIVE, 0.0).astype(BF16)
    for b in range(batch):
        masked_queries[b, :, 0:d] = query_rows(0, b)
        for g in range(group):
            masked_queries[b, g * here_rows : (g + 1) * here_rows, d : 2 * d] = row_mask

    @pl.loop(0, RING * RING)
    def _(i):
        for n, step in forward_steps.items():
            run_at(i == n, step)
        dp = pick(i, [f[0] for f in FORWARD])
        dq = pick(i, [f[1] for f in FORWARD])
        at = dp * RING + dq
        def softmax(b, span, scores):
            before = top_now[b, :, span]
            folded = jnp.max(scores.reshape(-1, 8, scores.shape[1]), axis=0)
            now = jnp.maximum(before, jnp.max(folded, axis=0, keepdims=True))
            top_now[b, :, span] = now
            tops[b, at, :, span] = now
            ratio = jnp.exp2((before - now) * factor)
            e = jnp.exp2(scores * factor - now[0:1] * factor)
            row_sum[b, :, span] = row_sum[b, :, span] * ratio + jnp.sum(e.reshape(-1, 8, e.shape[1]), axis=0)
            low = e.astype(BF16)
            weights[b, at, :, span] = low
            return ratio, low

        keys = [
            jnp.concatenate([cat(b, dp, dq, keys_at), mask_features(b, dp, dq)], axis=1) for b in range(batch)
        ]
        values_t = [cat(b, dp, dq, values_at).T for b in range(batch)]

        scores = [[nt(keys[b], masked_queries[b, span]) for span in tiles] for b in range(batch)]
        for b in range(batch):
            ratios = []
            for span, tile in zip(tiles, scores[b]):
                ratios.append(softmax(b, span, tile)[0][0:1])
            acc_t[b] = acc_t[b] * jnp.concatenate(ratios, axis=1) + nn(values_t[b], weights[b, at])

    laid_out(1)
    for b in range(batch):
        inverse = 1.0 / jnp.sum(row_sum[b], axis=0, keepdims=True)
        attended_t = acc_t[b] * inverse
        alive = lax.broadcasted_iota(jnp.int32, (here_rows, d), 0) + chip * here_rows < length_ref[0, b]
        alive = jnp.concatenate([jnp.where(alive, 1.0, 0.0)] * group, axis=0)
        live_grad = jnp.where(alive > 0.5, query_rows(1, b).astype(F32), 0.0)
        scaled_t = (live_grad.T * inverse).astype(BF16)
        delta_ref[b] = jnp.broadcast_to(
            jnp.sum(scaled_t.astype(F32) * attended_t, axis=0, keepdims=True), delta_ref.shape[1:]
        )
        douts_t[b] = scaled_t
        douts[b] = scaled_t.astype(F32).T.astype(BF16)
        attended = jnp.where(alive > 0.5, attended_t.T, 0.0).astype(BF16)
        rows_ref[1, b] = attended.reshape(rows_ref.shape[2:])
        acc_t[b] = jnp.zeros_like(acc_t[b])

    def away(n, target):
        return pltpu.make_async_copy(native.at[n], target.at[0], local_sem.at[4 + n])

    def leave(n):
        copies.send(("out", n), lambda: (rows_ref.at[1 - n, :, :, 1 - core], fin.at[n], sibling()))
        for g in range(group):
            native[n, :, :, head_lanes(core, g)] = jnp.swapaxes(rows_ref[1 - n, :, g, core], 0, 1)

    def settle_rows(n, target):
        copies.arrived(("out", n), fin.at[n], sibling())
        for g in range(group):
            native[n, :, :, head_lanes(1 - core, g)] = jnp.swapaxes(fin[n, :, g], 0, 1)
        away(n, target).start()

    leave(0)

    def add(into, other_ref):
        into[...] = (into[...].astype(F32) + other_ref[...].astype(F32)).astype(BF16)

    def far(k):
        for r in range(2):
            for n, direction in enumerate((1, 3)):

                def ends(r=r, n=n, direction=direction):
                    ref = total_at(r, BACK_P[k], 2).at[parts[n]]
                    return ref, far2.at[r, k, n], to(sources[r], 0, direction)

                copies.send(("back far2", r, k, n), ends)

    def near(k):
        for r in range(2):
            for n, direction in enumerate((1, 3)):
                copies.arrived(("back far2", r, k, n), far2.at[r, k, n], to(sources[r], 0, direction))
                add(total_at(r, BACK_P[k], direction).at[parts[n]], far2.at[r, k, n])

                def ends(r=r, n=n, direction=direction):
                    return total_at(r, BACK_P[k], direction), near2.at[r, k, n], to(sources[r], 0, direction)

                copies.send(("back near2", r, k, n), ends)

    def settle(k):
        for r in range(2):
            for n, direction in enumerate((1, 3)):
                copies.arrived(("back near2", r, k, n), near2.at[r, k, n], to(sources[r], 0, direction))
            into = total_at(r, BACK_P[k], 0)
            into[...] = (
                into[...].astype(F32) + near2[r, k, 0].astype(F32) + near2[r, k, 1].astype(F32)
            ).astype(BF16)

    def far_first():
        for r in range(2):
            for n, direction in enumerate((1, 3)):

                def ends(r=r, n=n, direction=direction):
                    return total_at(r, 2, 0).at[parts[n]], far1.at[r, n], to(sources[r], direction, 0)

                copies.send(("back far1", r, n), ends)

    def near_first(k):
        n, direction = k - 1, BACK_P[k]
        for r in range(2):
            copies.arrived(("back far1", r, n), far1.at[r, n], to(sources[r], direction, 0))
            add(total_at(r, direction, 0).at[parts[n]], far1.at[r, n])

            def ends(r=r):
                return total_at(r, direction, 0), near1.at[r, n], to(sources[r], direction, 0)

            copies.send(("back near1", r, n), ends)

    back_steps = {
        0: lambda: far(0),
        1: lambda: (far(1), settle_rows(0, att_final)),
        3: lambda: near(0),
        4: lambda: far(2),
        6: lambda: near(1),
        8: lambda: (far(3), settle(0), far_first()),
        10: lambda: near(2),
        11: lambda: (settle(1), near_first(1)),
        13: lambda: near(3),
        14: lambda: (settle(2), near_first(2)),
    }

    @pl.loop(0, RING * RING)
    def _(j):
        dp = pick(j, [BACK_P[f[0]] for f in BACKWARD])
        dq = pick(j, [f[1] for f in BACKWARD])
        at = dp * RING + dq
        key_terms, value_terms = [], []
        for b in range(batch):
            values = cat(b, dp, dq, values_at)
            for span in tiles:
                ratio = jnp.exp2((tops[b, at, :, span] - top_now[b, :, span]) * factor)[0:1]
                low = (weights[b, at, :, span].astype(F32) * ratio).astype(BF16)
                probs_low[b, :, span] = low
                grad_probs = nn(values, douts_t[b, :, span])
                grad_low = low.astype(F32) * (grad_probs - delta_ref[b, 0:1, span])
                weights[b, at, :, span] = grad_low.astype(BF16)
            value_terms.append(nn(probs_low[b], douts[b]))
            key_terms.append(nn(weights[b, at], query_rows(0, b)) * scale)
        for lanes, terms in ((keys_at, key_terms), (values_at, value_terms)):
            prefix = sum(terms)[CORES * pos :]
            for r in range(2):
                spot = total_at(r, dp, dq)
                for b in range(batch):
                    spot[b * pos : (b + 1) * pos, lanes] = terms[b][r * pos : (r + 1) * pos].astype(BF16)
                spot[ans_rows:block_rows, lanes] = prefix[r * 2 * pre_rows : (r + 1) * 2 * pre_rows].astype(BF16)
        for n, step in back_steps.items():
            run_at(j == n, step)

    @pl.loop(0, RING)
    def _(dp):
        for b in range(batch):
            keys = jnp.concatenate([cat(b, dp, dq, keys_at).T for dq in range(RING)], axis=1)
            grads = weights[b, pl.ds(dp * RING, RING)]
            acc_t[b] += nn(keys, grads.reshape(-1, rows))

    for b in range(batch):
        rows_ref[0, b] = (acc_t[b] * scale).T.astype(BF16).reshape(rows_ref.shape[2:])
    leave(1)
    settle(3)
    for r in (1, 0):
        for n, direction in enumerate((1, 3)):
            copies.arrived(("back near1", r, n), near1.at[r, n], to(sources[r], direction, 0))
        here = total_at(r, 0, 0)

        def final(area):
            return here[area].astype(F32) + near1[r, 0, area].astype(F32) + near1[r, 1, area].astype(F32)

        pre_swap[r, 0] = final(other).astype(BF16)
        if r == 1:
            copies.send(("pre", 1, 0), lambda: (pre_swap.at[1, 0], pre_got.at[1, 0], across(False)))
            pre_swap[1, 1] = final(mine).astype(BF16)
            copies.send(("pre", 1, 1), lambda: (pre_swap.at[1, 1], pre_got.at[1, 1], sibling()))
            ans_swap[...] = final(pl.ds(0, ans_rows)).astype(BF16)
            copies.send(("ans",), lambda: (ans_swap, ans_out.at[core], sibling()))
        else:
            copies.send(("pre", 0, 0), lambda: (pre_swap.at[0, 0], pre_got.at[0, 0], across(True)))
            pre_out[core] = final(mine)
            ans_out[core] = final(pl.ds(0, ans_rows)).astype(BF16)
    settle_rows(1, dq_final)
    copies.arrived(("pre", 1, 1), pre_got.at[1, 1], sibling())
    copies.arrived(("pre", 1, 0), pre_got.at[1, 0], across(False))
    pre_out[1 - core] = pre_got[1, 0].astype(F32) + pre_got[1, 1].astype(F32)
    copies.arrived(("pre", 0, 0), pre_got.at[0, 0], across(True))
    pre_out[core] = pre_out[core] + pre_got[0, 0].astype(F32)
    copies.arrived(("ans",), ans_out.at[1 - core], sibling())
    for n, (answer, prefix) in enumerate(((ak_final, pk_final), (av_final, pv_final))):
        lanes = slice(n * d, (n + 1) * d)
        for c in range(CORES):
            head = slice(c * d, (c + 1) * d)
            prefix[:, head] = pre_out[c, :, lanes]
            answer[0, :, :, head] = jnp.swapaxes(ans_out[c, :, lanes].reshape(-1, pos, d), 0, 1)
    away(0, att_final).wait()
    away(1, dq_final).wait()
    copies.finish()


def layer(lengths, limits, answer_keys, answer_values, prefix_keys, prefix_values, queries, grad_out):
    d = HEAD_DIM
    _, pos, batch, features = queries.shape
    group = features // d // CORES
    rows, width = group * CORES * pos, 2 * d
    ans_rows, pre_rows = batch * pos, prefix_keys.shape[0]
    block = ans_rows + 2 * pre_rows
    half = block // 2
    groups = RING * RING
    keys = CORES * (pos + 2 * pre_rows)
    vmem = pl.BlockSpec(memory_space=pltpu.VMEM)
    smem = pl.BlockSpec(memory_space=pltpu.SMEM)
    anywhere = pl.BlockSpec(memory_space=pl.ANY)
    tokens = jax.ShapeDtypeStruct(queries.shape, BF16)
    answers = jax.ShapeDtypeStruct(answer_keys.shape, BF16)
    prefix = jax.ShapeDtypeStruct(prefix_keys.shape, F32)
    per_head = (batch, group, pos, d)
    return pl.pallas_call(
        functools.partial(layer_kernel, group),
        out_shape=(tokens, tokens, answers, answers, prefix, prefix),
        in_specs=[smem] * 2 + [anywhere] * 6,
        out_specs=(anywhere, anywhere, vmem, vmem, vmem, vmem),
        scratch_shapes=[
            pltpu.VMEM((RING, RING, CORES, block, width), BF16),
            pltpu.VMEM((RING, RING, CORES, block, width), BF16),
            pltpu.VMEM((CORES, ans_rows, width), BF16),
            pltpu.VMEM((CORES, pre_rows, width), BF16),
            pltpu.VMEM((2,) + answer_keys.shape, BF16),
            pltpu.VMEM((2,) + prefix_keys.shape, BF16),
            pltpu.VMEM((2, pos, batch, features), BF16),
            pltpu.VMEM((2,) + per_head, BF16),
            pltpu.VMEM((2, batch, group, CORES, pos, d), BF16),
            pltpu.VMEM((batch, groups, keys, rows), BF16),
            pltpu.VMEM((batch, groups, 8, rows), F32),
            pltpu.VMEM((batch, 8, rows), F32),
            pltpu.VMEM((batch, 8, rows), F32),
            pltpu.VMEM((batch, d, rows), F32),
            pltpu.VMEM((batch, rows, d), BF16),
            pltpu.VMEM((batch, d, rows), BF16),
            pltpu.VMEM((batch, 8, rows), F32),
            pltpu.VMEM((batch, rows, 2 * d), BF16),
            pltpu.VMEM((batch, keys, rows), BF16),
            pltpu.VMEM((2,) + per_head, BF16),
            pltpu.VMEM((CORES, ans_rows, width), BF16),
            pltpu.VMEM((CORES, pre_rows, width), F32),
            pltpu.VMEM((CORES, RING, 2, half, width), BF16),
            pltpu.VMEM((CORES, RING, 2, block, width), BF16),
            pltpu.VMEM((CORES, 2, half, width), BF16),
            pltpu.VMEM((CORES, 2, block, width), BF16),
            pltpu.VMEM((ans_rows, width), BF16),
            pltpu.VMEM((2, 2, pre_rows, width), BF16),
            pltpu.VMEM((2, 2, pre_rows, width), BF16),
            pltpu.SemaphoreType.DMA((COPIES,)),
            pltpu.SemaphoreType.DMA((COPIES,)),
            pltpu.SemaphoreType.DMA((10,)),
        ],
        compiler_params=pltpu.CompilerParams(
            collective_id=0, has_side_effects=True, vmem_limit_bytes=60 * 1024 * 1024
        ),
        name="layer",
    )(lengths, limits, answer_keys, answer_values, prefix_keys, prefix_values, queries, grad_out)


def settle_kernel(count, *refs):
    ins, outs, held, sems = refs[:count], refs[count : 2 * count], refs[2 * count : 3 * count], refs[3 * count]
    takes = [pltpu.make_async_copy(ins[n], held[n], sems.at[n]) for n in range(count)]
    gives = [pltpu.make_async_copy(held[n], outs[n], sems.at[count + n]) for n in range(count)]
    for copy in takes:
        copy.start()
    for take, give in zip(takes, gives):
        take.wait()
        give.start()
    for copy in gives:
        copy.wait()


def settle_results(results):
    count = len(results)
    anywhere = pl.BlockSpec(memory_space=pl.ANY)
    return pl.pallas_call(
        functools.partial(settle_kernel, count),
        out_shape=tuple(jax.ShapeDtypeStruct(x.shape, x.dtype) for x in results),
        in_specs=[anywhere] * count,
        out_specs=(anywhere,) * count,
        scratch_shapes=[pltpu.VMEM(x.shape, x.dtype) for x in results]
        + [pltpu.SemaphoreType.DMA((2 * count,))],
        name="settle",
    )(*results)


def on_device(
    queries,
    answer_keys,
    answer_values,
    prefix_keys,
    prefix_values,
    grad_out,
    answer_length,
    prefix_limit,
):
    return settle_results(
        layer(
            answer_length,
            prefix_limit,
            answer_keys,
            answer_values,
            prefix_keys,
            prefix_values,
            queries,
            grad_out,
        )
    )


def solution(mesh):
    tokens = P("pair", "seq", None, "head")
    prefix = P(("pair", "seq"), "head")
    scalars = P("pair", None)
    return jax.shard_map(
        on_device,
        mesh=mesh,
        in_specs=(tokens, tokens, tokens, prefix, prefix, tokens, scalars, scalars),
        out_specs=(tokens, tokens, tokens, tokens, prefix, prefix),
        check_vma=False,
    )
```

time: 475 us -> 74.3 us (0.16)
  waiting for transfers between devices: 197 us -> 0 us
  matrix products: 106 us -> 0 us
  local copies, waits for them, and re-layouts: 89.4 us -> 0 us
  Pallas kernels: 0 us -> 73.5 us
  other arithmetic: 52.6 us -> 0 us
  between operations: 14.7 us -> 0.64 us
  starting transfers between devices: 11 us -> 0 us
    unnamed x4 -> x0, waiting for transfers between devices: 112 us -> none
    dot_general x70 -> x0, matrix products: 106 us -> none  [the longest x10 35.9 us: update(): jnp.einsum(forms[1], probs_low, value_block, preferred_element_type=jnp.f...]
    all_gather x2 -> x0, waiting for transfers between devices: 85.4 us -> none  [side_by_side(): lax.all_gather(both, axis, axis=dim, tiled=True)]
    pallas_call x0 -> x2, Pallas kernels: none -> 73.5 us  [the longest x1 71.4 us: layer(): pl.pallas_call(functools.partial(layer_kernel, group), out_shape=(tokens,...]
    another operation x6 -> x0, local copies, waits for them, and re-layouts: 20.9 us -> none  [the longest x2 9.79 us: sweep_keys(): value_rows.reshape((blocks_total, block_rows) + value_rows.shape[1:])]
    reduce_sum x13 -> x0, other arithmetic: 19.8 us -> none  [the longest x10 11.9 us: update(): jnp.sum(jnp.where(allowed, jnp.exp(masked - new_top[..., None]), 0.0), ax...]
    add x54 -> x0, other arithmetic: 19.6 us -> none  [the longest x18 11.6 us: prefix_allowed_keys(): places = first + lax.iota(jnp.int32, key_span)]
    unnamed x38 -> x0, local copies, waits for them, and re-layouts: 19.4 us -> none
  transfers between devices with their start and end apart: 5 -> 0, of which waited for: 3 -> 0; matrix products, arithmetic and copies ran while one was open for 19% -> 0% of each run, Pallas kernels for 0% -> 0%
where the time goes in v3:
time: 74.3 us; the launch traced here: 74.1 us
  Pallas kernels  73.5 us (99%)
    pallas_call x1, Pallas kernels, layer(): pl.pallas_call(functools.partial(layer_kernel, group), out_shape=(tokens,...  71.4 us
    pallas_call x1, Pallas kernels, settle_results(): pl.pallas_call(functools.partial(settle_kernel, count), out_shape=tuple((...  2.11 us

profile of v3, /device:TPU:1, one launch (start us, length us, event | category | flops | bytes accessed | tf_op | source)
XLA Modules:
  0.0 74.1 jit_solution(8893709944520451054)
XLA Ops:
  0.6 71.4 %layer.1 = (bf16[1,64,2,1792]{3,2,1,0:T(2,128)(2,1)}, bf16[1,64,2,1792]{3,2,1,0:T(2,128)(2,1)}, bf16[1,64,2,256]{3,2,1,0:T(2,128)(2,1)}, bf16[1,64,2,256]{3,2,1,...) custom-call(s32[1,2]{1,0:T(1,128)} %length_ref.1, s32[1,2]{1,0:T(1,128)} %limit_ref.1, ...), custom_call_target="tpu_custom_call" | custom-call | tf_op jit(solution)/shard_map/layer/pallas_call | solution.py:624
  72.0 2.1 %settle.1 = (bf16[1,64,2,1792]{3,2,1,0:T(2,128)(2,1)}, bf16[1,64,2,1792]{3,2,1,0:T(2,128)(2,1)}, bf16[1,64,2,256]{3,2,1,0:T(2,128)(2,1)}, bf16[1,64,2,256]{3,2,1...) custom-call(bf16[1,64,2,1792]{3,2,1,0:T(2,128)(2,1)} %get-tuple-element.12.refs_0_, ...), custom_call_target="tpu_custom_call" | custom-call | tf_op jit(solution)/shard_map/settle/pallas_call | solution.py:686

commit v4 on v3

--- a/solution.py
+++ b/solution.py
@@ -124,7 +124,7 @@
     return lax.dot_general(a, b, (((1,), (1,)), ((), ())), preferred_element_type=F32)
 
 
-COPIES = 104
+COPIES = 120
 ORDER = (0, 3, 1, 2)
 FORWARD = (
     (0, 0), (3, 0), (1, 0), (0, 3), (0, 1), (2, 0), (3, 3), (3, 1),
@@ -258,15 +258,16 @@
                 ("two", r, 0, direction, piece), lambda direction=direction: (source, ref, to(sources[r], 0, direction))
             )
 
-    def spread(k):
+    def spread(k, piece):
         for r in range(2):
             for direction in (1, 3):
 
                 def ends(r=r, direction=direction):
                     ref = held_at(r, ORDER[k], 0)
+                    ref = ref if piece == 2 else ref.at[pieces[piece]]
                     return ref, ref, to(sources[r], 0, direction)
 
-                copies.send(("two", r, k, direction, 2), ends)
+                copies.send(("two", r, k, direction, piece), ends)
 
     def head_lanes(c, g):
         return pl.ds(pl.multiple_of((c * group + g) * d, d), d)
@@ -295,23 +296,21 @@
     own(1, 1)
     laid_out(0)
 
-    def first_neighbours():
+    def first_neighbours(piece):
         for direction in (1, 3):
             back = (-direction) % RING
             for r in range(2):
-                for piece in range(2):
-                    copies.arrived(
-                        ("one", r, direction, piece),
-                        held_at(r, back, 0).at[pieces[piece]],
-                        to(sources[r], direction, 0),
-                    )
+                copies.arrived(
+                    ("one", r, direction, piece), held_at(r, back, 0).at[pieces[piece]], to(sources[r], direction, 0)
+                )
 
                 def ends(r=r, direction=direction, back=back):
                     ref = held_at(r, back, 0).at[parts[direction // 2]]
                     return ref, ref, to(sources[r], direction, 0)
 
-                copies.send(("far", r, direction), ends)
-            spread(ORDER.index(back))
+                if piece == 1:
+                    copies.send(("far", r, direction), ends)
+            spread(ORDER.index(back), piece)
 
     def first_far():
         for r in range(2):
@@ -319,14 +318,14 @@
                 copies.arrived(
                     ("far", r, direction), held_at(r, 2, 0).at[parts[direction // 2]], to(sources[r], direction, 0)
                 )
-        spread(3)
+        spread(3, 2)
 
     def second_neighbours(k):
         for direction in (1, 3):
             back = (-direction) % RING
             for r in range(2):
                 here = held_at(r, ORDER[k], back)
-                for piece in range(2) if k == 0 else (2,):
+                for piece in range(2) if k < 3 else (2,):
                     area = here if piece == 2 else here.at[pieces[piece]]
                     copies.arrived(("two", r, k, direction, piece), area, to(sources[r], 0, direction))
 
@@ -343,7 +342,7 @@
                 copies.arrived(("far2", r, k, direction), here.at[parts[direction // 2]], to(sources[r], 0, direction))
 
     forward_steps = {
-        1: first_neighbours,
+        1: lambda: (first_neighbours(0), first_neighbours(1)),
         2: lambda: lay_out(1),
         3: lambda: second_neighbours(0),
         5: first_far,
@@ -447,19 +446,17 @@
         rows_ref[1, b] = attended.reshape(rows_ref.shape[2:])
         acc_t[b] = jnp.zeros_like(acc_t[b])
 
-    def away(n, target):
-        return pltpu.make_async_copy(native.at[n], target.at[0], local_sem.at[4 + n])
+    rows_final = (att_final, dq_final)
 
     def leave(n):
         copies.send(("out", n), lambda: (rows_ref.at[1 - n, :, :, 1 - core], fin.at[n], sibling()))
         for g in range(group):
-            native[n, :, :, head_lanes(core, g)] = jnp.swapaxes(rows_ref[1 - n, :, g, core], 0, 1)
-
-    def settle_rows(n, target):
+            rows_final[n][0, :, :, head_lanes(core, g)] = jnp.swapaxes(rows_ref[1 - n, :, g, core], 0, 1)
+
+    def settle_rows(n):
         copies.arrived(("out", n), fin.at[n], sibling())
         for g in range(group):
-            native[n, :, :, head_lanes(1 - core, g)] = jnp.swapaxes(fin[n, :, g], 0, 1)
-        away(n, target).start()
+            rows_final[n][0, :, :, head_lanes(1 - core, g)] = jnp.swapaxes(fin[n, :, g], 0, 1)
 
     leave(0)
 
@@ -476,21 +473,27 @@
 
                 copies.send(("back far2", r, k, n), ends)
 
-    def near(k):
+    tail_pieces = (pieces[1], pieces[0])
+
+    def near(k, piece=None):
         for r in range(2):
             for n, direction in enumerate((1, 3)):
-                copies.arrived(("back far2", r, k, n), far2.at[r, k, n], to(sources[r], 0, direction))
-                add(total_at(r, BACK_P[k], direction).at[parts[n]], far2.at[r, k, n])
+                if piece != 1:
+                    copies.arrived(("back far2", r, k, n), far2.at[r, k, n], to(sources[r], 0, direction))
+                    add(total_at(r, BACK_P[k], direction).at[parts[n]], far2.at[r, k, n])
 
                 def ends(r=r, n=n, direction=direction):
-                    return total_at(r, BACK_P[k], direction), near2.at[r, k, n], to(sources[r], 0, direction)
-
-                copies.send(("back near2", r, k, n), ends)
+                    source, target = total_at(r, BACK_P[k], direction), near2.at[r, k, n]
+                    if piece is not None:
+                        source, target = source.at[tail_pieces[piece]], target.at[tail_pieces[piece]]
+                    return source, target, to(sources[r], 0, direction)
+
+                copies.send(("back near2", r, k, n, piece), ends)
 
     def settle(k):
         for r in range(2):
             for n, direction in enumerate((1, 3)):
-                copies.arrived(("back near2", r, k, n), near2.at[r, k, n], to(sources[r], 0, direction))
+                copies.arrived(("back near2", r, k, n, None), near2.at[r, k, n], to(sources[r], 0, direction))
             into = total_at(r, BACK_P[k], 0)
             into[...] = (
                 into[...].astype(F32) + near2[r, k, 0].astype(F32) + near2[r, k, 1].astype(F32)
@@ -505,28 +508,44 @@
 
                 copies.send(("back far1", r, n), ends)
 
-    def near_first(k):
+    def near_first(k, piece):
         n, direction = k - 1, BACK_P[k]
         for r in range(2):
-            copies.arrived(("back far1", r, n), far1.at[r, n], to(sources[r], direction, 0))
-            add(total_at(r, direction, 0).at[parts[n]], far1.at[r, n])
+            if piece == 0:
+                copies.arrived(("back far1", r, n), far1.at[r, n], to(sources[r], direction, 0))
+                add(total_at(r, direction, 0).at[parts[n]], far1.at[r, n])
 
             def ends(r=r):
-                return total_at(r, direction, 0), near1.at[r, n], to(sources[r], direction, 0)
-
-            copies.send(("back near1", r, n), ends)
+                area = tail_pieces[piece]
+                return total_at(r, direction, 0).at[area], near1.at[r, n, area], to(sources[r], direction, 0)
+
+            copies.send(("back near1", r, n, piece), ends)
+
+    def finish_piece(piece):
+        for r in range(2):
+            for n, direction in enumerate((1, 3)):
+                area = tail_pieces[piece]
+                copies.arrived(("back near2", r, 3, n, piece), near2.at[r, 3, n, area], to(sources[r], 0, direction))
+                copies.arrived(("back near1", r, n, piece), near1.at[r, n, area], to(sources[r], direction, 0))
+
+    def final(r, area):
+        parts_in = (near2[r, 3, 0, area], near2[r, 3, 1, area], near1[r, 0, area], near1[r, 1, area])
+        value = total_at(r, 0, 0)[area].astype(F32)
+        for part in parts_in:
+            value = value + part.astype(F32)
+        return value
 
     back_steps = {
         0: lambda: far(0),
-        1: lambda: (far(1), settle_rows(0, att_final)),
+        1: lambda: (far(1), settle_rows(0)),
         3: lambda: near(0),
         4: lambda: far(2),
         6: lambda: near(1),
         8: lambda: (far(3), settle(0), far_first()),
         10: lambda: near(2),
-        11: lambda: (settle(1), near_first(1)),
-        13: lambda: near(3),
-        14: lambda: (settle(2), near_first(2)),
+        11: lambda: (settle(1), near_first(1, 0)),
+        13: lambda: near(3, 0),
+        14: lambda: (settle(2), near_first(2, 0), near(3, 1), near_first(1, 1), near_first(2, 1)),
     }
 
     @pl.loop(0, RING * RING)
@@ -556,6 +575,17 @@
         for n, step in back_steps.items():
             run_at(j == n, step)
 
+    finish_piece(0)
+    for r in (1, 0):
+        pre_swap[r, 0] = final(r, other).astype(BF16)
+        if r == 1:
+            copies.send(("pre", 1, 0), lambda: (pre_swap.at[1, 0], pre_got.at[1, 0], across(False)))
+            pre_swap[1, 1] = final(1, mine).astype(BF16)
+            copies.send(("pre", 1, 1), lambda: (pre_swap.at[1, 1], pre_got.at[1, 1], sibling()))
+        else:
+            copies.send(("pre", 0, 0), lambda: (pre_swap.at[0, 0], pre_got.at[0, 0], across(True)))
+            pre_out[core] = final(0, mine)
+
     @pl.loop(0, RING)
     def _(dp):
         for b in range(batch):
@@ -566,27 +596,11 @@
     for b in range(batch):
         rows_ref[0, b] = (acc_t[b] * scale).T.astype(BF16).reshape(rows_ref.shape[2:])
     leave(1)
-    settle(3)
-    for r in (1, 0):
-        for n, direction in enumerate((1, 3)):
-            copies.arrived(("back near1", r, n), near1.at[r, n], to(sources[r], direction, 0))
-        here = total_at(r, 0, 0)
-
-        def final(area):
-            return here[area].astype(F32) + near1[r, 0, area].astype(F32) + near1[r, 1, area].astype(F32)
-
-        pre_swap[r, 0] = final(other).astype(BF16)
-        if r == 1:
-            copies.send(("pre", 1, 0), lambda: (pre_swap.at[1, 0], pre_got.at[1, 0], across(False)))
-            pre_swap[1, 1] = final(mine).astype(BF16)
-            copies.send(("pre", 1, 1), lambda: (pre_swap.at[1, 1], pre_got.at[1, 1], sibling()))
-            ans_swap[...] = final(pl.ds(0, ans_rows)).astype(BF16)
-            copies.send(("ans",), lambda: (ans_swap, ans_out.at[core], sibling()))
-        else:
-            copies.send(("pre", 0, 0), lambda: (pre_swap.at[0, 0], pre_got.at[0, 0], across(True)))
-            pre_out[core] = final(mine)
-            ans_out[core] = final(pl.ds(0, ans_rows)).astype(BF16)
-    settle_rows(1, dq_final)
+    finish_piece(1)
+    ans_swap[...] = final(1, pieces[0]).astype(BF16)
+    copies.send(("ans",), lambda: (ans_swap, ans_out.at[core], sibling()))
+    ans_out[core] = final(0, pieces[0]).astype(BF16)
+    settle_rows(1)
     copies.arrived(("pre", 1, 1), pre_got.at[1, 1], sibling())
     copies.arrived(("pre", 1, 0), pre_got.at[1, 0], across(False))
     pre_out[1 - core] = pre_got[1, 0].astype(F32) + pre_got[1, 1].astype(F32)
@@ -599,8 +613,6 @@
             head = slice(c * d, (c + 1) * d)
             prefix[:, head] = pre_out[c, :, lanes]
             answer[0, :, :, head] = jnp.swapaxes(ans_out[c, :, lanes].reshape(-1, pos, d), 0, 1)
-    away(0, att_final).wait()
-    away(1, dq_final).wait()
     copies.finish()
 
 
@@ -617,15 +629,15 @@
     vmem = pl.BlockSpec(memory_space=pltpu.VMEM)
     smem = pl.BlockSpec(memory_space=pltpu.SMEM)
     anywhere = pl.BlockSpec(memory_space=pl.ANY)
-    tokens = jax.ShapeDtypeStruct(queries.shape, BF16)
-    answers = jax.ShapeDtypeStruct(answer_keys.shape, BF16)
-    prefix = jax.ShapeDtypeStruct(prefix_keys.shape, F32)
+    tokens = pltpu.VMEM(queries.shape, BF16)
+    answers = pltpu.VMEM(answer_keys.shape, BF16)
+    prefix = pltpu.VMEM(prefix_keys.shape, F32)
     per_head = (batch, group, pos, d)
     return pl.pallas_call(
         functools.partial(layer_kernel, group),
         out_shape=(tokens, tokens, answers, answers, prefix, prefix),
         in_specs=[smem] * 2 + [anywhere] * 6,
-        out_specs=(anywhere, anywhere, vmem, vmem, vmem, vmem),
+        out_specs=(vmem,) * 6,
         scratch_shapes=[
             pltpu.VMEM((RING, RING, CORES, block, width), BF16),
             pltpu.VMEM((RING, RING, CORES, block, width), BF16),
@@ -661,37 +673,31 @@
             pltpu.SemaphoreType.DMA((10,)),
         ],
         compiler_params=pltpu.CompilerParams(
-            collective_id=0, has_side_effects=True, vmem_limit_bytes=60 * 1024 * 1024
+            collective_id=0, has_side_effects=True, vmem_limit_bytes=58 * 1024 * 1024
         ),
         name="layer",
     )(lengths, limits, answer_keys, answer_values, prefix_keys, prefix_values, queries, grad_out)
 
 
 def settle_kernel(count, *refs):
-    ins, outs, held, sems = refs[:count], refs[count : 2 * count], refs[2 * count : 3 * count], refs[3 * count]
-    takes = [pltpu.make_async_copy(ins[n], held[n], sems.at[n]) for n in range(count)]
-    gives = [pltpu.make_async_copy(held[n], outs[n], sems.at[count + n]) for n in range(count)]
-    for copy in takes:
+    ins, outs, sems = refs[:count], refs[count : 2 * count], refs[2 * count]
+    gives = [pltpu.make_async_copy(ins[n], outs[n], sems.at[n]) for n in range(count)]
+    for copy in gives:
         copy.start()
-    for take, give in zip(takes, gives):
-        take.wait()
-        give.start()
     for copy in gives:
         copy.wait()
 
 
 def settle_results(results):
     count = len(results)
-    anywhere = pl.BlockSpec(memory_space=pl.ANY)
     return pl.pallas_call(
         functools.partial(settle_kernel, count),
         out_shape=tuple(jax.ShapeDtypeStruct(x.shape, x.dtype) for x in results),
-        in_specs=[anywhere] * count,
-        out_specs=(anywhere,) * count,
-        scratch_shapes=[pltpu.VMEM(x.shape, x.dtype) for x in results]
-        + [pltpu.SemaphoreType.DMA((2 * count,))],
+        in_specs=[pl.BlockSpec(memory_space=pltpu.VMEM)] * count,
+        out_specs=(pl.BlockSpec(memory_space=pl.ANY),) * count,
+        scratch_shapes=[pltpu.SemaphoreType.DMA((count,))],
         name="settle",
-    )(*results)
+    )(*[pltpu.with_memory_space_constraint(x, pltpu.VMEM) for x in results])
 
 
 def on_device(

time: 74.3 us -> 72.2 us (0.972)
  Pallas kernels: 73.5 us -> 71.5 us
    pallas_call x1, Pallas kernels: 2.11 us -> 1.04 us  [settle_results(): pl.pallas_call(functools.partial(settle_kernel, count), out_shape=tuple((...]
    pallas_call x1, Pallas kernels: 71.4 us -> 70.4 us  [layer(): pl.pallas_call(functools.partial(layer_kernel, group), out_shape=(tokens,...]
where the time goes in v4:
time: 72.2 us; the launch traced here: 72.1 us
  Pallas kernels  71.5 us (99%)
    pallas_call x1, Pallas kernels, layer(): pl.pallas_call(functools.partial(layer_kernel, group), out_shape=(tokens,...  70.4 us

profile of v4, /device:TPU:1, one launch (start us, length us, event | category | flops | bytes accessed | tf_op | source)
XLA Modules:
  0.0 72.1 jit_solution(11438094722700672309)
XLA Ops:
  0.6 70.4 %layer.1 = (bf16[1,64,2,1792]{3,2,1,0:T(2,128)(2,1)S(1)}, bf16[1,64,2,1792]{3,2,1,0:T(2,128)(2,1)S(1)}, bf16[1,64,2,256]{3,2,1,0:T(2,128)(2,1)S(1)}, bf16[1,64,2...) custom-call(s32[1,2]{1,0:T(1,128)} %length_ref.1, s32[1,2]{1,0:T(1,128)} %limit_ref.1, ...), custom_call_target="tpu_custom_call" | custom-call | tf_op jit(solution)/shard_map/layer/pallas_call | solution.py:636
  71.1 1.0 %settle.1 = (bf16[1,64,2,1792]{3,2,1,0:T(2,128)(2,1)}, bf16[1,64,2,1792]{3,2,1,0:T(2,128)(2,1)}, bf16[1,64,2,256]{3,2,1,0:T(2,128)(2,1)}, bf16[1,64,2,256]{3,2,1...) custom-call(bf16[1,64,2,1792]{3,2,1,0:T(2,128)(2,1)S(1)} %get-tuple-element.12.refs_0_, ...), custom_call_target="tpu_custom_call" | custom-call | tf_op jit(solution)/shard_map/settle/pallas_call | solution.py:693

commit v5 on v4

--- a/solution.py
+++ b/solution.py
@@ -246,17 +246,13 @@
     copies.send(("pair", 0), lambda: (staged_pre.at[core], there.at[mine], across(True)))
     copies.send(("pair", 1), lambda: (staged_pre.at[1 - core], there.at[mine], across(False)))
 
-    def own(r, piece):
+    def own(r, piece, axis):
         ref = held_at(r, 0, 0).at[pieces[piece]]
         source = staged_ans.at[core] if (r, piece) == (0, 0) else ref
         for direction in (1, 3):
-            copies.send(
-                ("one", r, direction, piece), lambda direction=direction: (source, ref, to(sources[r], direction, 0))
-            )
-        for direction in (1, 3):
-            copies.send(
-                ("two", r, 0, direction, piece), lambda direction=direction: (source, ref, to(sources[r], 0, direction))
-            )
+            key = ("one", r, direction, piece) if axis == 0 else ("two", r, 0, direction, piece)
+            step = (direction, 0) if axis == 0 else (0, direction)
+            copies.send(key, lambda step=step: (source, ref, to(sources[r], *step)))
 
     def spread(k, piece):
         for r in range(2):
@@ -283,17 +279,21 @@
     def laid_out(n):
         copies.arrived(("q", n), rows_ref.at[n, :, :, 1 - core], sibling())
 
-    own(0, 0)
+    own(0, 0, 0)
+    own(0, 0, 1)
     lay_out(0)
     copies.arrived(("sib", 0), held_at(1, 0, 0).at[pieces[0]], sibling())
-    own(1, 0)
+    own(1, 0, 0)
+    own(1, 0, 1)
     for copy in loads:
         copy.wait()
     copies.arrived(("pair", 0), held_at(0, 0, 0).at[other], across(True))
-    own(0, 1)
+    own(0, 1, 0)
     copies.arrived(("sib", 1), held_at(1, 0, 0).at[mine], sibling())
     copies.arrived(("pair", 1), held_at(1, 0, 0).at[other], across(False))
-    own(1, 1)
+    own(1, 1, 0)
+    own(0, 1, 1)
+    own(1, 1, 1)
     laid_out(0)
 
     def first_neighbours(piece):
@@ -342,8 +342,7 @@
                 copies.arrived(("far2", r, k, direction), here.at[parts[direction // 2]], to(sources[r], 0, direction))
 
     forward_steps = {
-        1: lambda: (first_neighbours(0), first_neighbours(1)),
-        2: lambda: lay_out(1),
+        1: lambda: (first_neighbours(0), lay_out(1), first_neighbours(1)),
         3: lambda: second_neighbours(0),
         5: first_far,
         6: lambda: second_neighbours(1),

time: 72.2 us -> 71.7 us (level)
  no operation moved by 1% of the time
where the time goes in v5:
time: 71.7 us; the launch traced here: 71.6 us
  Pallas kernels  70.9 us (99%)
    pallas_call x1, Pallas kernels, layer(): pl.pallas_call(functools.partial(layer_kernel, group), out_shape=(tokens,...  69.9 us

profile of v5, /device:TPU:1, one launch (start us, length us, event | category | flops | bytes accessed | tf_op | source)
XLA Modules:
  0.0 71.6 jit_solution(9707809237526380734)
XLA Ops:
  0.6 69.9 %layer.1 = (bf16[1,64,2,1792]{3,2,1,0:T(2,128)(2,1)S(1)}, bf16[1,64,2,1792]{3,2,1,0:T(2,128)(2,1)S(1)}, bf16[1,64,2,256]{3,2,1,0:T(2,128)(2,1)S(1)}, bf16[1,64,2...) custom-call(s32[1,2]{1,0:T(1,128)} %length_ref.1, s32[1,2]{1,0:T(1,128)} %limit_ref.1, ...), custom_call_target="tpu_custom_call" | custom-call | tf_op jit(solution)/shard_map/layer/pallas_call | solution.py:635
  70.5 1.0 %settle.1 = (bf16[1,64,2,1792]{3,2,1,0:T(2,128)(2,1)}, bf16[1,64,2,1792]{3,2,1,0:T(2,128)(2,1)}, bf16[1,64,2,256]{3,2,1,0:T(2,128)(2,1)}, bf16[1,64,2,256]{3,2,1...) custom-call(bf16[1,64,2,1792]{3,2,1,0:T(2,128)(2,1)S(1)} %get-tuple-element.12.refs_0_, ...), custom_call_target="tpu_custom_call" | custom-call | tf_op jit(solution)/shard_map/settle/pallas_call | solution.py:692
